TPU v7x, 256 devices: a whole 4x4x8 slice. The times are simulated.
256 devices in a mesh: band: 16 (over z, y_lo), grid: 16 (over x, y_hi, core).
Axes of the slice: x: 4, y: 4 (y_hi: 2, y_lo: 2; y = y_hi * 2 + y_lo), z: 8, core: 2. Of those that a mesh axis runs over, the one named last changes fastest.
Arguments:
- orbitals: bfloat16 [16, 128, 128, 128], P('band', 'grid'), may hold values from -3 to 3
- trial_vectors: bfloat16 [2, 16, 128, 128, 128], P(None, 'band', 'grid'), may hold values from -6 to 6
- alda_kernel: float32 [128, 128, 128], P('grid'), may hold values from -2 to -0.5
- local_potential: float32 [128, 128, 128], P('grid'), may hold values from -2 to 1
- band_energies: float32 [16], P('band'), may hold values from -1.5 to -0.2
Outputs:
- sigma_real: float32 [2, 16, 128, 128, 128], P(None, 'band', 'grid')
- sigma_imag: float32 [2, 16, 128, 128, 128], P(None, 'band', 'grid')
All inputs are finite; a program needn't handle non-finite values.
Results may differ from a plain program's by a relative error of at most 0.0003.
Values sent between devices are 32-bit elements; how exact they have to be, the bound alone decides.
No kernel may reach another device: no remote copies, remote signals or barrier semaphores. Data moves between devices by JAX's collectives and lax.ppermute only.
A program may use at most 64 MiB of HBM per device.

v0:
```python
import math

import jax
import jax.numpy as jnp
from jax import lax
from jax.sharding import PartitionSpec as P

box_length = 30.0
highest = lax.Precision.HIGHEST


def cut_along(array, dim, peers):
    before, after = (array.shape[:dim], array.shape[dim + 1 :])
    return jnp.moveaxis(array.reshape(*before, peers, -1, *after), dim, 0)


def sent_and_summed(array, axis, dim):
    pieces = cut_along(array, dim, lax.axis_size(axis))
    arrived = lax.all_to_all(pieces, axis, split_axis=0, concat_axis=0, tiled=True)
    return arrived.sum(axis=0)


def sent_to_all(array, axis):
    copies = jnp.broadcast_to(array, (lax.axis_size(axis), *array.shape))
    return lax.all_to_all(copies, axis, split_axis=0, concat_axis=0, tiled=True)


def laid_out(pieces, dim):
    pieces = jnp.moveaxis(pieces, 0, dim)
    lengths = pieces.shape
    return pieces.reshape(*lengths[:dim], lengths[dim] * lengths[dim + 1], *lengths[dim + 2 :])


def collect(array, axis, dim):
    pieces = sent_to_all(array, axis)
    return laid_out(pieces, dim)


def tables(length):
    positions = jnp.arange(length, dtype=jnp.int32)
    wrapped = positions[:, None] * positions[None, :] % length
    angles = wrapped.astype(jnp.float32) * (2.0 * math.pi / length)
    return (jnp.cos(angles), jnp.sin(angles))


def contract(pattern, left_operand, right_operand):
    return jnp.einsum(pattern, left_operand, right_operand, precision=highest)


def rotate(pattern, real_part, imag_part, cosine_table, sine_table, orient):
    new_real = contract(pattern, real_part, cosine_table) - orient * contract(
        pattern, imag_part, sine_table
    )
    new_imag = contract(pattern, imag_part, cosine_table) + orient * contract(
        pattern, real_part, sine_table
    )
    return (new_real, new_imag)


def rotate_real(pattern, real_part, cosine_table, sine_table, orient):
    return (
        contract(pattern, real_part, cosine_table),
        orient * contract(pattern, real_part, sine_table),
    )


def frequency(length, offset, extent):
    positions = offset + jnp.arange(extent, dtype=jnp.int32)
    signed = jnp.where(2 * positions < length, positions, positions - length)
    return signed.astype(jnp.float32)


def coulomb(first_freq, second_freq, third_freq):
    squared = (
        first_freq[:, None, None] ** 2
        + second_freq[None, :, None] ** 2
        + third_freq[None, None, :] ** 2
    )
    scaled = box_length**2 / math.pi / jnp.maximum(squared, 1.0)
    return jnp.where(squared > 0, scaled, 0.0)


def potential_split(density_share, cosine_table, sine_table, length):
    real_part, imag_part = rotate_real(
        "kxyz,zg->kxgy", density_share, cosine_table, sine_table, -1.0
    )
    arrived = lax.all_to_all(
        jnp.stack((real_part, imag_part)), "band", split_axis=3, concat_axis=4, tiled=True
    )
    real_part, imag_part = rotate(
        "kxzy,yg->kgzx", arrived[0], arrived[1], cosine_table, sine_table, -1.0
    )
    arrived = lax.all_to_all(
        jnp.stack((real_part, imag_part)), "grid", split_axis=2, concat_axis=4, tiled=True
    )
    real_part, imag_part = rotate(
        "kyzx,xg->kyzg", arrived[0], arrived[1], cosine_table, sine_table, -1.0
    )
    rows_here = real_part.shape[1]
    planes_here = real_part.shape[2]
    kernel = coulomb(
        frequency(length, lax.axis_index("grid") * rows_here, rows_here),
        frequency(length, lax.axis_index("band") * planes_here, planes_here),
        frequency(length, 0, length),
    )
    real_part = real_part * kernel[None]
    imag_part = imag_part * kernel[None]
    real_part, imag_part = rotate(
        "kyzg,gx->kyzx", real_part, imag_part, cosine_table, sine_table, 1.0
    )
    arrived = lax.all_to_all(
        jnp.stack((real_part, imag_part)), "grid", split_axis=4, concat_axis=2, tiled=True
    )
    real_part, imag_part = rotate(
        "kgzx,gy->kxzy", arrived[0], arrived[1], cosine_table, sine_table, 1.0
    )
    arrived = lax.all_to_all(
        jnp.stack((real_part, imag_part)), "band", split_axis=4, concat_axis=3, tiled=True
    )
    restored = contract("kxgy,gz->kxyz", arrived[0], cosine_table) - contract(
        "kxgy,gz->kxyz", arrived[1], sine_table
    )
    return restored / float(length**3)


def per_device(orbitals, trial_vectors, alda_kernel, local_potential, band_energies):
    length = orbitals.shape[2]
    cosine_table, sine_table = tables(length)
    orbital_wide = orbitals.astype(jnp.float32)
    trial_wide = trial_vectors.astype(jnp.float32)
    partial_value = 2.0 * jnp.sum(trial_wide * orbital_wide[None], axis=1)
    density_share = sent_and_summed(partial_value, "band", 2)
    row_count = density_share.shape[2]
    kernel_rows = lax.dynamic_slice_in_dim(
        alda_kernel, lax.axis_index("band") * row_count, row_count, 1
    )
    hartree = potential_split(density_share, cosine_table, sine_table, length)
    potential = collect(hartree + kernel_rows[None] * density_share, "band", 2)
    weight = local_potential[None] - band_energies[:, None, None, None]
    fields = potential[:, None] * orbital_wide[None] + weight[None] * trial_wide
    trial_count = trial_vectors.shape[0]
    band_count = trial_vectors.shape[1]
    norm_factor = float(length) ** (-1.5)
    flattened = fields.reshape((trial_count * band_count,) + fields.shape[2:])
    real_part, imag_part = rotate_real("mxyz,zg->mxyg", flattened, cosine_table, sine_table, -1.0)
    real_part, imag_part = rotate(
        "mxyz,yg->mgzx", real_part, imag_part, cosine_table, sine_table, -1.0
    )
    received = lax.all_to_all(
        jnp.stack((real_part, imag_part)), "grid", split_axis=2, concat_axis=4, tiled=True
    )
    real_part, imag_part = rotate(
        "myzx,xg->myzg", received[0], received[1], cosine_table, sine_table, -1.0
    )
    results = jnp.stack((real_part * norm_factor, imag_part * norm_factor))
    results = results.reshape((2, trial_count, band_count) + results.shape[2:])
    return (results[0], results[1])


def solution(mesh):
    placed = (
        P("band", "grid", None, None),
        P(None, "band", "grid", None, None),
        P("grid", None, None),
        P("grid", None, None),
        P("band"),
    )
    return jax.shard_map(
        per_device,
        mesh=mesh,
        in_specs=placed,
        out_specs=(P(None, "band", "grid", None, None), P(None, "band", "grid", None, None)),
        check_vma=False,
    )
```

profile of v0, /device:TPU:1, one launch (start us, length us, event | category | flops | bytes accessed | tf_op | source)
XLA Modules:
  0.0 250.4 jit_solution(17965347319409852565)
XLA Ops:
  4.0 10.1 %all-to-all-start = ((f32[16,2,8,8,128]{4,3,2,1,0:T(8,128)}), f32[16,2,8,8,128]{4,3,2,1,0:T(8,128)S(1)}, u32[]{:S(2)}, u32[]{:S(2)}) async-start(f32[16,2,8,8,128]{4,3,2,1,0:T(8,128)} %copy.72), calls=%async_computation | async-start | bytes 2097152 | tf_op jit(solution)/shard_map/all_to_all | solution.py:19
  14.1 25.4 %all-to-all-done = f32[16,2,8,8,128]{4,3,2,1,0:T(8,128)S(1)} async-done(((f32[16,2,8,8,128]{4,3,2,1,0:T(8,128)}), f32[16,2,8,8,128]{4,3,2,1,0:T(8,128)S(1)}, u32[]{:S(2)}, u32[]{:S(2)}) %all-to-all-start) | async-done | bytes 1048608 | tf_op jit(solution)/shard_map/all_to_all | solution.py:19
  44.1 6.8 %all-to-all-start.1 = ((f32[16,1,2048]{2,1,0:T(1,128)}), f32[16,1,2048]{2,1,0:T(1,128)S(1)}, u32[]{:S(2)}, u32[]{:S(2)}) async-start(f32[16,1,2048]{2,1,0:T(1,128)} %reshape.151), calls=%async_computation.1 | async-start | bytes 262144 | tf_op jit(solution)/shard_map/all_to_all | solution.py:87
  51.0 8.4 %all-to-all-done.1 = f32[16,1,2048]{2,1,0:T(1,128)S(1)} async-done(((f32[16,1,2048]{2,1,0:T(1,128)}), f32[16,1,2048]{2,1,0:T(1,128)S(1)}, u32[]{:S(2)}, u32[]{:S(2)}) %all-to-all-start.1) | async-done | bytes 131104 | tf_op jit(solution)/shard_map/all_to_all | solution.py:87
  60.8 2.5 reshape.152
  63.3 2.7 %copy.115 = f32[2,2,8,16,8,8]{4,3,5,2,1,0:T(8,128)S(1)} copy(f32[2,2,8,16,8,8]{5,2,1,0,4,3:T(8,128)} %bitcast.234) | data formatting | bytes 262144 | tf_op jit(solution)/shard_map/all_to_all | solution.py:87
  76.6 9.7 %all-to-all-start.2 = ((f32[16,1,2048]{2,1,0:T(1,128)}), f32[16,1,2048]{2,1,0:T(1,128)S(1)}, u32[]{:S(2)}, u32[]{:S(2)}) async-start(f32[16,1,2048]{2,1,0:T(1,128)} %reshape.153), calls=%async_computation.2 | async-start | bytes 262144 | tf_op jit(solution)/shard_map/all_to_all | solution.py:93
  86.4 7.4 %all-to-all-done.2 = f32[16,1,2048]{2,1,0:T(1,128)S(1)} async-done(((f32[16,1,2048]{2,1,0:T(1,128)}), f32[16,1,2048]{2,1,0:T(1,128)S(1)}, u32[]{:S(2)}, u32[]{:S(2)}) %all-to-all-start.2) | async-done | bytes 131104 | tf_op jit(solution)/shard_map/all_to_all | solution.py:93
  94.8 2.5 reshape.154
  97.3 3.0 %copy.116 = f32[2,2,16,8,8,8]{3,2,5,4,1,0:T(8,128)S(1)} copy(f32[2,2,16,8,8,8]{4,5,1,0,3,2:T(8,128)} %bitcast.236) | data formatting | bytes 262144 | tf_op jit(solution)/shard_map/all_to_all | solution.py:93
  101.8 2.2 copy.79
  112.6 10.8 %all_to_all.85 = f32[16,1,2048]{2,1,0:T(1,128)S(1)} all-to-all(f32[16,1,2048]{2,1,0:T(1,128)S(1)} %reshape.155), channel_id=1, replica_groups=mesh['band'=16,'grid'=16] {'grid'}, dimensions={0} | all-to-all | bytes 262144 | tf_op jit(solution)/shard_map/all_to_all | solution.py:111
  124.3 2.5 reshape.156
  126.8 2.7 %copy.117 = f32[2,2,8,8,16,8]{5,4,3,2,1,0:T(8,128)S(1)} copy(f32[2,2,8,8,16,8]{3,2,1,0,5,4:T(8,128)} %bitcast.238) | data formatting | bytes 262144 | tf_op jit(solution)/shard_map/all_to_all | solution.py:111
  130.9 2.1 copy.84
  140.3 3.5 %all-to-all-start.4 = ((f32[16,1,2048]{2,1,0:T(1,128)}), f32[16,1,2048]{2,1,0:T(1,128)S(1)}, u32[]{:S(2)}, u32[]{:S(2)}) async-start(f32[16,1,2048]{2,1,0:T(1,128)} %reshape.157), calls=%async_computation.4 | async-start | bytes 262144 | tf_op jit(solution)/shard_map/all_to_all | solution.py:117
  143.9 8.7 %all-to-all-done.4 = f32[16,1,2048]{2,1,0:T(1,128)S(1)} async-done(((f32[16,1,2048]{2,1,0:T(1,128)}), f32[16,1,2048]{2,1,0:T(1,128)S(1)}, u32[]{:S(2)}, u32[]{:S(2)}) %all-to-all-start.4) | async-done | bytes 131104 | tf_op jit(solution)/shard_map/all_to_all | solution.py:117
  153.4 2.5 reshape.158
  155.9 3.0 %copy.118 = f32[2,2,8,8,16,8]{5,4,3,2,1,0:T(8,128)S(1)} copy(f32[2,2,8,8,16,8]{2,3,1,0,5,4:T(8,128)} %bitcast.240) | data formatting | bytes 262144 | tf_op jit(solution)/shard_map/all_to_all | solution.py:117
  166.2 4.1 %all-to-all-start.5 = ((f32[16,2,8,8,128]{4,3,2,1,0:T(8,128)}), f32[16,2,8,8,128]{4,3,2,1,0:T(8,128)S(1)}, u32[]{:S(2)}, u32[]{:S(2)}) async-start(f32[16,2,8,8,128]{4,3,2,1,0:T(8,128)} %broadcast_in_dim.3), calls=%async_computation.5 | async-start | bytes 2097152 | tf_op jit(solution)/shard_map/all_to_all | solution.py:25
  171.0 23.7 %all-to-all-done.5 = f32[16,2,8,8,128]{4,3,2,1,0:T(8,128)S(1)} async-done(((f32[16,2,8,8,128]{4,3,2,1,0:T(8,128)}), f32[16,2,8,8,128]{4,3,2,1,0:T(8,128)S(1)}, u32[]{:S(2)}, u32[]{:S(2)}) %all-to-all-start.5) | async-done | bytes 1048608 | tf_op jit(solution)/shard_map/all_to_all | solution.py:25
  203.9 36.1 %all_to_all.86 = f32[2,2,128,128,8]{3,4,1,0,2:T(8,128)S(1)} all-to-all(f32[2,2,128,128,8]{3,4,1,0,2:T(8,128)S(1)} %copy.94), channel_id=1, replica_groups=mesh['band'=16,'grid'=16] {'grid'}, dimensions={2} | all-to-all | bytes 4194304 | tf_op jit(solution)/shard_map/all_to_all | solution.py:149
  244.3 2.9 %fusion.9 = f32[2,1,8,128,128]{4,3,2,1,0:T(8,128)} fusion(f32[2,8,128,128]{3,2,1,0:T(8,128)S(1)} %fusion.27, f32[1,2,8,128,16,8]{3,5,2,4,1,0:T(8,128)S(1)} %get-tuple-element.11), kind=kOutput, calls=%fused_computation.15 | convolution fusion | flops 403668992 | bytes 3145728 | tf_op jit(solution)/shard_map/myzx,xg->myzg/dot_general | solution.py:47
  247.3 2.9 %fusion.7 = f32[2,1,8,128,128]{4,3,2,1,0:T(8,128)} fusion(f32[2,8,128,128]{3,2,1,0:T(8,128)S(1)} %fusion.31, f32[1,2,8,128,16,8]{3,5,2,4,1,0:T(8,128)S(1)} %get-tuple-element.10), kind=kOutput, calls=%fused_computation.13 | convolution fusion | flops 403668992 | bytes 3145728 | tf_op jit(solution)/shard_map/myzx,xg->myzg/dot_general | solution.py:47
  (96 shorter events, 62.3 us)
Async XLA Ops:
  0.6 143.2 %copy-start = (f32[8,128,128]{2,1,0:T(8,128)S(1)}, f32[8,128,128]{2,1,0:T(8,128)}, u32[]{:S(2)}) copy-start(f32[8,128,128]{2,1,0:T(8,128)} %param.7) | copy-start | bytes 1572868
  4.0 35.5 %all-to-all-start = ((f32[16,2,8,8,128]{4,3,2,1,0:T(8,128)}), f32[16,2,8,8,128]{4,3,2,1,0:T(8,128)S(1)}, u32[]{:S(2)}, u32[]{:S(2)}) async-start(f32[16,2,8,8,128]{4,3,2,1,0:T(8,128)} %copy.72), calls=%async_computation | async-start | bytes 2097152 | tf_op jit(solution)/shard_map/all_to_all | solution.py:19
  44.1 15.2 %all-to-all-start.1 = ((f32[16,1,2048]{2,1,0:T(1,128)}), f32[16,1,2048]{2,1,0:T(1,128)S(1)}, u32[]{:S(2)}, u32[]{:S(2)}) async-start(f32[16,1,2048]{2,1,0:T(1,128)} %reshape.151), calls=%async_computation.1 | async-start | bytes 262144 | tf_op jit(solution)/shard_map/all_to_all | solution.py:87
  67.5 3.0 %copy-start.5 = (f32[1,2,8,8,16,8]{3,4,5,2,1,0:T(8,128)S(1)}, f32[1,2,8,8,16,8]{3,4,5,2,1,0:T(8,128)}, u32[]{:S(2)}) copy-start(f32[1,2,8,8,16,8]{3,4,5,2,1,0:T(8,128)} %get-tuple-element.19) | copy-start | bytes 196612
  76.6 17.2 %all-to-all-start.2 = ((f32[16,1,2048]{2,1,0:T(1,128)}), f32[16,1,2048]{2,1,0:T(1,128)S(1)}, u32[]{:S(2)}, u32[]{:S(2)}) async-start(f32[16,1,2048]{2,1,0:T(1,128)} %reshape.153), calls=%async_computation.2 | async-start | bytes 262144 | tf_op jit(solution)/shard_map/all_to_all | solution.py:93
  101.8 3.2 %copy-start.6 = (f32[1,2,8,8,16,8]{2,4,5,3,1,0:T(8,128)S(1)}, f32[1,2,8,8,16,8]{2,4,5,3,1,0:T(8,128)}, u32[]{:S(2)}) copy-start(f32[1,2,8,8,16,8]{2,4,5,3,1,0:T(8,128)} %get-tuple-element.17) | copy-start | bytes 196612
  130.9 3.5 %copy-start.3 = (f32[1,2,16,8,8,8]{5,2,4,3,1,0:T(8,128)S(1)}, f32[1,2,16,8,8,8]{5,2,4,3,1,0:T(8,128)}, u32[]{:S(2)}) copy-start(f32[1,2,16,8,8,8]{5,2,4,3,1,0:T(8,128)} %get-tuple-element.14) | copy-start | bytes 196612
  140.3 12.2 %all-to-all-start.4 = ((f32[16,1,2048]{2,1,0:T(1,128)}), f32[16,1,2048]{2,1,0:T(1,128)S(1)}, u32[]{:S(2)}, u32[]{:S(2)}) async-start(f32[16,1,2048]{2,1,0:T(1,128)} %reshape.157), calls=%async_computation.4 | async-start | bytes 262144 | tf_op jit(solution)/shard_map/all_to_all | solution.py:117
  160.5 3.0 %copy-start.4 = (f32[1,2,8,16,8,8]{5,3,4,2,1,0:T(8,128)S(1)}, f32[1,2,8,16,8,8]{5,3,4,2,1,0:T(8,128)}, u32[]{:S(2)}) copy-start(f32[1,2,8,16,8,8]{5,3,4,2,1,0:T(8,128)} %get-tuple-element.12) | copy-start | bytes 196612
  164.1 6.8 %copy-start.7 = (f32[8,128,128]{2,1,0:T(8,128)S(1)}, f32[8,128,128]{2,1,0:T(8,128)}, u32[]{:S(2)}) copy-start(f32[8,128,128]{2,1,0:T(8,128)} %param.8) | copy-start | bytes 1572868
  165.1 29.6 %copy-start.2 = (bf16[2,1,8,128,128]{4,3,2,1,0:T(8,128)(2,1)S(1)}, bf16[2,1,8,128,128]{4,3,2,1,0:T(8,128)(2,1)}, u32[]{:S(2)}) copy-start(bf16[2,1,8,128,128]{4,3,2,1,0:T(8,128)(2,1)} %param.6) | copy-start | bytes 1572868
  166.2 28.5 %all-to-all-start.5 = ((f32[16,2,8,8,128]{4,3,2,1,0:T(8,128)}), f32[16,2,8,8,128]{4,3,2,1,0:T(8,128)S(1)}, u32[]{:S(2)}, u32[]{:S(2)}) async-start(f32[16,2,8,8,128]{4,3,2,1,0:T(8,128)} %broadcast_in_dim.3), calls=%async_computation.5 | async-start | bytes 2097152 | tf_op jit(solution)/shard_map/all_to_all | solution.py:25
  244.3 5.9 %copy-start.1 = (f32[8,128,128]{2,1,0:T(8,128)S(1)}, f32[8,128,128]{2,1,0:T(8,128)}, u32[]{:S(2)}) copy-start(f32[8,128,128]{2,1,0:T(8,128)} %param.7) | copy-start | bytes 1572868
where the time goes:
time: 254 us; the launch traced here: 250 us
  waiting for transfers between devices  73.5 us (29%)
  local copies, waits for them, and re-layouts  60.6 us (24%)
  blocking collectives  46.8 us (18%)
  starting transfers between devices  34.2 us (13%)
  matrix products  26.7 us (11%)
  other arithmetic  6.46 us (3%)
    all_to_all x1, blocking collectives, per_device(): lax.all_to_all(jnp.stack((real_part, imag_part)), 'grid', split_axis=2, c...  36.1 us
    all_to_all x1, waiting for transfers between devices, sent_and_summed(): lax.all_to_all(pieces, axis, split_axis=0, concat_axis=0, tiled=True)  25.4 us
    dot_general x26, matrix products, contract(): return jnp.einsum(pattern, left_operand, right_operand, precision=highest)  24.9 us
    all_to_all x1, waiting for transfers between devices, sent_to_all(): return lax.all_to_all(copies, axis, split_axis=0, concat_axis=0, tiled=True)  23.7 us
    unnamed x24, local copies, waits for them, and re-layouts  16.3 us
    slice x7, local copies, waits for them, and re-layouts, potential_split(): arrived[0]  11.5 us
    all_to_all x1, blocking collectives, potential_split(): lax.all_to_all(jnp.stack((real_part, imag_part)), 'grid', split_axis=4, c...  10.8 us
    all_to_all x1, starting transfers between devices, sent_and_summed(): lax.all_to_all(pieces, axis, split_axis=0, concat_axis=0, tiled=True)  10.1 us
  transfers between devices with their start and end apart: 5, of which 5 were waited for; matrix products, arithmetic and copies ran while one was open for 0% of the time, Pallas kernels for 0%

commit v1 on v0

v1 whole, which is shorter than its diff:
```python
import functools
import math

import jax
import jax.numpy as jnp
import numpy as np
from jax import lax
from jax.experimental import pallas as pl
from jax.experimental.pallas import tpu as pltpu
from jax.sharding import PartitionSpec as P

box_length = 30.0
NARROW = jnp.bfloat16
WIDE = jnp.float32


def halves(table):
    high = table.astype(np.float32).astype(jnp.bfloat16)
    low = (table - high.astype(np.float64)).astype(np.float32).astype(jnp.bfloat16)
    return np.stack([high, low])


def waves(rows, columns, period):
    wrapped = np.outer(np.asarray(rows), np.asarray(columns)) % period
    angles = wrapped.astype(np.float64) * (2.0 * math.pi / period)
    return np.cos(angles), np.sin(angles)


@functools.cache
def make_tables(length, parts):
    share = length // parts
    cosine, sine = waves(range(length), range(length), length)
    norm = float(length) ** -1.5
    out = {}
    out["share_forward"] = halves(np.concatenate([cosine, -sine], 0))
    out["share_back"] = halves(np.concatenate([cosine, -sine], 0))
    out["field_z"] = halves(np.concatenate([cosine, -sine], 1))
    out["field_y"] = halves(np.block([[cosine, sine], [-sine, cosine]]))
    out["field_x"] = halves(np.block([[cosine, -sine], [sine, cosine]]) * norm)
    pieces = np.arange(parts)
    outer, inner = np.repeat(pieces, parts), np.tile(pieces, parts)
    turns = np.outer(outer, outer) + np.outer(inner, inner)
    angles = 2.0 * math.pi * (turns % parts) / parts
    out["plane_rows"] = halves(np.concatenate([np.cos(angles), -np.sin(angles)], 0))
    steps = np.arange(share)
    first, second = np.repeat(steps, share), np.tile(steps, share)
    turns = np.outer(outer, second) + np.outer(inner, first)
    angles = 2.0 * math.pi * turns / length
    out["twist"] = np.stack(
        [np.tile(np.cos(angles), (1, 2)), np.tile(-np.sin(angles), (1, 2))]
    ).astype(np.float32)
    turns = np.outer(first, first) + np.outer(second, second)
    angles = 2.0 * math.pi * (turns % share) / share
    real, imag = np.cos(angles), -np.sin(angles)
    out["plane_lanes"] = halves(np.block([[real, imag], [-imag, real]]))
    out["plane_lanes_back"] = halves(np.block([[real, -imag], [imag, real]]))
    return out


def split(value):
    high = value.astype(NARROW)
    return high, (value - high.astype(WIDE)).astype(NARROW)


def mul(left, right, dims=((1,), (0,))):
    return lax.dot_general(left, right, (dims, ((), ())), preferred_element_type=WIDE)


def product(left, right, dims=((1,), (0,))):
    left_high, left_low = left
    right_high, right_low = right
    return (
        mul(left_high, right_high, dims)
        + mul(left_low, right_high, dims)
        + mul(left_high, right_low, dims)
    )


def pair(ref):
    return ref[0], ref[1]


def density_kernel(orbital_ref, trial_ref, out_ref):
    for x in range(orbital_ref.shape[1]):
        orbital = orbital_ref[0, x].astype(WIDE)
        for k in range(trial_ref.shape[0]):
            value = 2.0 * (trial_ref[k, 0, x].astype(WIDE) * orbital)
            out_ref[:, k, x] = value.reshape(out_ref.shape[0], *out_ref.shape[3:])


def density(orbitals, trials, parts):
    bands, rows, length, _ = orbitals.shape
    count = trials.shape[0]
    share = length // parts
    step = 2
    return pl.pallas_call(
        density_kernel,
        grid=(rows // step,),
        out_shape=jax.ShapeDtypeStruct((parts, count, rows, share, length), WIDE),
        in_specs=[
            pl.BlockSpec((1, step, length, length), lambda i: (0, i, 0, 0)),
            pl.BlockSpec((count, 1, step, length, length), lambda i: (0, 0, i, 0, 0)),
        ],
        out_specs=pl.BlockSpec((parts, count, step, share, length), lambda i: (0, 0, i, 0, 0)),
        name="density",
    )(orbitals, trials)


def share_forward_kernel(pieces_ref, table_ref, share_ref, out_ref):
    total = pieces_ref[0]
    for i in range(1, pieces_ref.shape[0]):
        total = total + pieces_ref[i]
    share_ref[...] = total
    length = total.shape[1]
    points = total.shape[0] // 2
    turned = product(pair(table_ref), split(total), ((1,), (1,)))
    for k in range(2):
        columns = slice(k * points, (k + 1) * points)
        out_ref[k * length : (k + 1) * length, :] = jnp.concatenate(
            [turned[:length, columns], turned[length:, columns]], axis=1
        )


def times_i(value):
    half = value.shape[1] // 2
    return jnp.concatenate([-value[:, half:], value[:, :half]], axis=1)


def plane_kernel(pieces_ref, kernel_ref, rows_ref, twist_ref, lanes_ref, back_ref, out_ref):
    count = pieces_ref.shape[0]
    rows = pair(rows_ref)
    turned = product(rows, split(pieces_ref[...]))
    value = turned[:count] + times_i(turned[count:])
    value = value * twist_ref[0] + times_i(value) * twist_ref[1]
    value = product(split(value), pair(lanes_ref))
    value = value * kernel_ref[...]
    value = product(split(value), pair(back_ref))
    value = value * twist_ref[0] - times_i(value) * twist_ref[1]
    turned = product(rows, split(value))
    out_ref[...] = turned[:count] - times_i(turned[count:])


def share_back_kernel(pieces_ref, table_ref, share_ref, alda_ref, out_ref):
    length = table_ref.shape[2]
    points = share_ref.shape[0] // 2
    rows = []
    for k in range(2):
        turned = pieces_ref[k * length : (k + 1) * length, :].T
        rows.append(jnp.concatenate([turned[:points], turned[points:]], axis=1))
    value = product(split(jnp.concatenate(rows, axis=0)), pair(table_ref))
    alda = jnp.concatenate([alda_ref[...], alda_ref[...]], axis=0)
    value = value + alda * share_ref[...]
    for i in range(out_ref.shape[0]):
        out_ref[i] = value


def field_kernel(
    energy_ref, potential_ref, orbital_ref, trial_ref, local_ref, z_ref, y_ref, out_ref
):
    length = orbital_ref.shape[2]
    parts = potential_ref.shape[0]
    energy = energy_ref[0]
    for x in range(orbital_ref.shape[1]):
        orbital = orbital_ref[0, x].astype(WIDE)
        weight = local_ref[x] - energy
        fields = []
        for k in range(2):
            potential = potential_ref[:, k, x].reshape(length, length)
            fields.append(potential * orbital + weight * trial_ref[k, 0, x].astype(WIDE))
        turned = product(split(jnp.concatenate(fields, axis=0)), pair(z_ref))
        real = jnp.concatenate([turned[:length, :length], turned[length:, :length]], axis=1)
        imag = jnp.concatenate([turned[:length, length:], turned[length:, length:]], axis=1)
        turned = product(pair(y_ref), split(jnp.concatenate([real, imag], axis=0)))
        for k in range(2):
            for part in range(2):
                block = turned[part * length : (part + 1) * length, k * length : (k + 1) * length]
                out_ref[:, k, part, x] = block.reshape(parts, length // parts, length)


def final_kernel(pieces_ref, x_ref, real_ref, imag_ref):
    length = real_ref.shape[-1]
    share = real_ref.shape[2]
    table = pair(x_ref)
    for k in range(2):
        for b in range(share):
            parts = []
            for part in range(2):
                start = (k * 2 + part) * share * share + b
                block = pieces_ref[:, pl.ds(start, share, stride=share), :]
                parts.append(block.reshape(length, length))
            turned = product(split(jnp.concatenate(parts, axis=0).T), table)
            real_ref[k, 0, b] = turned[:, :length]
            imag_ref[k, 0, b] = turned[:, length:]


def signed(positions, length):
    return jnp.where(2 * positions < length, positions, positions - length).astype(WIDE)


def plane_coulomb(c, length, parts):
    share = length // parts
    row = lax.broadcasted_iota(jnp.int32, (parts * parts, 2 * share * share), 0)
    lane = lax.broadcasted_iota(jnp.int32, (parts * parts, 2 * share * share), 1)
    lane = lane % (share * share)
    a = row % parts + parts * (lane // share)
    b = row // parts + parts * (lane % share)
    squared = signed(a, length) ** 2 + signed(b, length) ** 2 + signed(c, length) ** 2
    scaled = box_length**2 / math.pi / jnp.maximum(squared, 1.0)
    return jnp.where(squared > 0, scaled, 0.0) / float(length**3)


def call(body, shapes, name):
    return pl.pallas_call(
        body,
        out_shape=jax.tree.map(lambda s: jax.ShapeDtypeStruct(s, WIDE), shapes, is_leaf=lambda s: isinstance(s, tuple) and isinstance(s[0], int)),
        name=name,
    )


def exchange(array, axes):
    return lax.all_to_all(array, axes, split_axis=0, concat_axis=0, tiled=True)


def per_device(orbitals, trials, alda_kernel, local_potential, band_energies):
    length = orbitals.shape[2]
    parts = lax.axis_size("band")
    share = length // parts
    points = share * share
    count = trials.shape[0]
    everyone = ("band", "grid")
    tables = {name: jnp.asarray(table) for name, table in make_tables(length, parts).items()}
    me = lax.axis_index("band")
    here = me * parts + lax.axis_index("grid")
    kernel = plane_coulomb(here % length, length, parts)
    alda = lax.dynamic_slice_in_dim(alda_kernel, me * share, share, 1).reshape(points, length)

    pieces = density(orbitals, trials, parts).reshape(parts, count * points, length)
    pieces = exchange(pieces, "band")
    density_share, planes = call(
        share_forward_kernel,
        [(count * points, length), (count * length, 2 * points)],
        "share_forward",
    )(pieces, tables["share_forward"])
    planes = exchange(planes.reshape(-1, 1, 2 * points), everyone).reshape(-1, 2 * points)
    planes = call(plane_kernel, planes.shape, "plane")(
        planes,
        kernel,
        tables["plane_rows"],
        tables["twist"],
        tables["plane_lanes"],
        tables["plane_lanes_back"],
    )
    planes = exchange(planes.reshape(-1, 1, 2 * points), everyone).reshape(-1, 2 * points)
    potential = call(share_back_kernel, (parts, count * points, length), "share_back")(
        planes, tables["share_back"], density_share, alda
    )
    potential = exchange(potential, "band").reshape(parts, count, share, share, length)

    step = 2
    fields = pl.pallas_call(
        field_kernel,
        grid=(share // step,),
        out_shape=jax.ShapeDtypeStruct((parts, count, 2, share, share, length), WIDE),
        in_specs=[
            pl.BlockSpec(memory_space=pltpu.SMEM),
            pl.BlockSpec((parts, count, step, share, length), lambda i: (0, 0, i, 0, 0)),
            pl.BlockSpec((1, step, length, length), lambda i: (0, i, 0, 0)),
            pl.BlockSpec((count, 1, step, length, length), lambda i: (0, 0, i, 0, 0)),
            pl.BlockSpec((step, length, length), lambda i: (i, 0, 0)),
            pl.BlockSpec((2, length, 2 * length), lambda i: (0, 0, 0)),
            pl.BlockSpec((2, 2 * length, 2 * length), lambda i: (0, 0, 0)),
        ],
        out_specs=pl.BlockSpec(
            (parts, count, 2, step, share, length), lambda i: (0, 0, 0, i, 0, 0)
        ),
        name="field",
    )(
        band_energies,
        potential,
        orbitals,
        trials,
        local_potential,
        tables["field_z"],
        tables["field_y"],
    )
    received = exchange(fields.reshape(parts, count * 2 * points, length), "grid")
    shape = (count, 1, share, length, length)
    return tuple(call(final_kernel, [shape, shape], "final")(received, tables["field_x"]))


def solution(mesh):
    placed = (
        P("band", "grid", None, None),
        P(None, "band", "grid", None, None),
        P("grid", None, None),
        P("grid", None, None),
        P("band"),
    )
    return jax.shard_map(
        per_device,
        mesh=mesh,
        in_specs=placed,
        out_specs=(P(None, "band", "grid", None, None), P(None, "band", "grid", None, None)),
        check_vma=False,
    )
```

time: 254 us -> 171 us (0.67); the launches traced: 250 us -> 171 us
  local copies, waits for them, and re-layouts: 60.6 us -> 3.87 us
  matrix products: 26.7 us -> 0 us
  Pallas kernels: 0 us -> 21.6 us
  blocking collectives: 46.8 us -> 36.3 us
  other arithmetic: 6.46 us -> 0.97 us
  starting transfers between devices: 34.2 us -> 31.5 us
    dot_general x26 -> x0, matrix products: 24.9 us -> none  [contract(): return jnp.einsum(pattern, left_operand, right_operand, precision=highest)]
    pallas_call x0 -> x6, Pallas kernels: none -> 21.6 us  [the longest x1 6.05 us: per_device(): pl.pallas_call(field_kernel, grid=(share // step,), out_shape=jax.ShapeDt...]
    slice x13 -> x0, local copies, waits for them, and re-layouts: 17.5 us -> none  [the longest x7 11.5 us: potential_split(): arrived[0]]
    unnamed x24 -> x10, local copies, waits for them, and re-layouts: 16.3 us -> 3.26 us
    all_to_all x6 -> x0, local copies, waits for them, and re-layouts: 12.1 us -> none  [the longest x2 3.22 us: potential_split(): lax.all_to_all(jnp.stack((real_part, imag_part)), 'band', split_axis=3, c...]
    all_to_all x2 -> x1, blocking collectives: 46.8 us -> 36.3 us  [exchange(): return lax.all_to_all(array, axes, split_axis=0, concat_axis=0, tiled=True)]
    another operation x5 -> x0, local copies, waits for them, and re-layouts: 8.5 us -> none  [the longest x4 7.28 us: potential_split(): jnp.stack((real_part, imag_part))]
    squeeze x8 -> x0, local copies, waits for them, and re-layouts: 3.98 us -> none  [the longest x4 1.99 us: potential_split(): arrived[0]]
  transfers between devices with their start and end apart: 5 -> 4, of which waited for: 5 -> 4; matrix products, arithmetic and copies ran while one was open for 0% -> 1% of each run, Pallas kernels for 0% -> 0%
where the time goes in v1:
time: 171 us
  waiting for transfers between devices  75.2 us (44%)
  blocking collectives  36.3 us (21%)
  starting transfers between devices  31.5 us (18%)
  Pallas kernels  21.6 us (13%)
  local copies, waits for them, and re-layouts  3.87 us (2%)
    all_to_all x4, waiting for transfers between devices, exchange(): return lax.all_to_all(array, axes, split_axis=0, concat_axis=0, tiled=True)  75.2 us
    all_to_all x1, blocking collectives, exchange(): return lax.all_to_all(array, axes, split_axis=0, concat_axis=0, tiled=True)  36.3 us
    all_to_all x4, starting transfers between devices, exchange(): return lax.all_to_all(array, axes, split_axis=0, concat_axis=0, tiled=True)  31.5 us
    pallas_call x1, Pallas kernels, per_device(): pl.pallas_call(field_kernel, grid=(share // step,), out_shape=jax.ShapeDt...  6.05 us
    pallas_call x1, Pallas kernels, per_device(): call(final_kernel, [shape, shape], 'final')(received, tables['field_x'])  3.97 us
    pallas_call x1, Pallas kernels, per_device(): call(plane_kernel, planes.shape, 'plane')  3.62 us
    pallas_call x1, Pallas kernels, density(): pl.pallas_call(density_kernel, grid=(rows // step,), out_shape=jax.ShapeD...  3.44 us
  transfers between devices with their start and end apart: 4, of which 4 were waited for; matrix products, arithmetic and copies ran while one was open for 1% of the time, Pallas kernels for 0%

profile of v1, /device:TPU:1, one launch (start us, length us, event | category | flops | bytes accessed | tf_op | source)
XLA Modules:
  0.0 170.8 jit_solution(4114892164326661083)
XLA Ops:
  0.6 0.0 copy-start
  0.6 3.4 %density.1 = f32[16,2,8,8,128]{4,3,2,1,0:T(8,128)} custom-call(bf16[1,8,128,128]{3,2,1,0:T(8,128)(2,1)} %orbital_ref.3, bf16[2,1,8,128,128]{4,3,2,1,0:T(8,128)(2,1)} %trial_ref.3), custom_call_target="tpu_custom_call" | custom-call | tf_op jit(solution)/shard_map/density/pallas_call | solution.py:96
  4.1 10.1 %all-to-all-start = ((f32[16,128,128]{2,1,0:T(8,128)}), f32[16,128,128]{2,1,0:T(8,128)S(1)}, u32[]{:S(2)}, u32[]{:S(2)}) async-start(f32[16,128,128]{2,1,0:T(8,128)} %bitcast.15), calls=%async_computation | async-start | bytes 2097152 | tf_op jit(solution)/shard_map/all_to_all | solution.py:221
  14.3 25.4 %all-to-all-done.pieces_ref = f32[16,128,128]{2,1,0:T(8,128)S(1)} async-done(((f32[16,128,128]{2,1,0:T(8,128)}), f32[16,128,128]{2,1,0:T(8,128)S(1)}, u32[]{:S(2)}, u32[]{:S(2)}) %all-to-all-start) | async-done | bytes 1048608 | tf_op jit(solution)/shard_map/all_to_all | solution.py:221
  39.6 0.0 copy-start.2
  39.6 1.0 copy-done.2
  40.6 2.2 %share_forward.1 = (f32[128,128]{1,0:T(8,128)}, f32[256,128]{1,0:T(8,128)}) custom-call(f32[16,128,128]{2,1,0:T(8,128)} %copy-done.2, bf16[2,256,128]{2,1,0:T(8,128)(2,1)} %constant.118.clone.table_ref), custom_call_target="tpu_custom_call" | custom-call | tf_op jit(solution)/shard_map/share_forward/pallas_call | solution.py:239
  42.8 12.3 %all-to-all-start.1 = ((f32[256,1,128]{2,1,0:T(1,128)}), f32[256,1,128]{2,1,0:T(1,128)S(1)}, u32[]{:S(2)}, u32[]{:S(2)}) async-start(f32[256,1,128]{2,1,0:T(1,128)} %bitcast.19), calls=%async_computation.1 | async-start | bytes 262144 | tf_op jit(solution)/shard_map/all_to_all | solution.py:221
  55.2 0.9 select_multiply_fusion.kernel_ref
  56.1 12.1 %all-to-all-done.1 = f32[256,1,128]{2,1,0:T(1,128)S(1)} async-done(((f32[256,1,128]{2,1,0:T(1,128)}), f32[256,1,128]{2,1,0:T(1,128)S(1)}, u32[]{:S(2)}, u32[]{:S(2)}) %all-to-all-start.1) | async-done | bytes 131104 | tf_op jit(solution)/shard_map/all_to_all | solution.py:221
  68.2 0.7 copy-done.3
  68.9 3.6 %plane.1 = f32[256,128]{1,0:T(8,128)} custom-call(f32[256,128]{1,0:T(8,128)} %bitcast.16, f32[256,128]{1,0:T(8,128)} %select_multiply_fusion.kernel_ref, bf16[2,512,256]{2,1,0:T(8,128)(2,1)} %constant.122.clone.rows_ref, f32[2,256,128]{2,1,0:T(8,128)} %constant.123.clone.twist_ref, bf16[2,128,128]{2,1,0:T(8,128)(2,1)} %constant.124.clone.lanes_ref, ...), custom_call_target="tpu_custom_call" | custom-call | tf_op jit(solution)/shard_map/plane/pallas_call | solution.py:245
  72.5 5.4 %all-to-all-start.2 = ((f32[256,1,128]{2,1,0:T(1,128)}), f32[256,1,128]{2,1,0:T(1,128)S(1)}, u32[]{:S(2)}, u32[]{:S(2)}) async-start(f32[256,1,128]{2,1,0:T(1,128)} %bitcast.17), calls=%async_computation.2 | async-start | bytes 262144 | tf_op jit(solution)/shard_map/all_to_all | solution.py:221
  77.9 0.0 copy-done
  78.0 0.6 dynamic-slice_bitcast_fusion.alda_ref
  78.6 12.6 %all-to-all-done.2 = f32[256,1,128]{2,1,0:T(1,128)S(1)} async-done(((f32[256,1,128]{2,1,0:T(1,128)}), f32[256,1,128]{2,1,0:T(1,128)S(1)}, u32[]{:S(2)}, u32[]{:S(2)}) %all-to-all-start.2) | async-done | bytes 131104 | tf_op jit(solution)/shard_map/all_to_all | solution.py:221
  91.2 0.7 copy-done.4
  91.8 2.3 %share_back.1 = f32[16,128,128]{2,1,0:T(8,128)} custom-call(f32[256,128]{1,0:T(8,128)} %bitcast.18, bf16[2,256,128]{2,1,0:T(8,128)(2,1)} %constant.118.clone.table_ref, f32[128,128]{1,0:T(8,128)} %get-tuple-element.5.share_ref, f32[64,128]{1,0:T(8,128)} %dynamic-slice_bitcast_fusion.alda_ref), custom_call_target="tpu_custom_call" | custom-call | tf_op jit(solution)/shard_map/share_back/pallas_call | solution.py:254
  94.1 3.7 %all-to-all-start.3 = ((f32[16,128,128]{2,1,0:T(8,128)}), f32[16,128,128]{2,1,0:T(8,128)S(1)}, u32[]{:S(2)}, u32[]{:S(2)}) async-start(f32[16,128,128]{2,1,0:T(8,128)} %share_back.1), calls=%async_computation.3 | async-start | bytes 2097152 | tf_op jit(solution)/shard_map/all_to_all | solution.py:221
  98.4 25.2 %all-to-all-done.3 = f32[16,128,128]{2,1,0:T(8,128)S(1)} async-done(((f32[16,128,128]{2,1,0:T(8,128)}), f32[16,128,128]{2,1,0:T(8,128)S(1)}, u32[]{:S(2)}, u32[]{:S(2)}) %all-to-all-start.3) | async-done | bytes 1048608 | tf_op jit(solution)/shard_map/all_to_all | solution.py:221
  123.6 1.0 copy-done.1
  124.5 6.1 %field.1 = f32[16,2,2,8,8,128]{5,4,3,2,1,0:T(8,128)} custom-call(f32[1]{0:T(128)S(6)} %copy.18.energy_ref, f32[16,2,8,8,128]{4,3,2,1,0:T(8,128)} %bitcast.14, bf16[1,8,128,128]{3,2,1,0:T(8,128)(2,1)} %orbital_ref.3, bf16[2,1,8,128,128]{4,3,2,1,0:T(8,128)(2,1)} %trial_ref.3, f32[8,128,128]{2,1,0:T(8,128)} %local_ref.1, ...), custom_call_target="tpu_custom_call" | custom-call | tf_op jit(solution)/shard_map/field/pallas_call | solution.py:260
  130.6 36.3 %all_to_all.25.pieces_ref = f32[16,256,128]{2,1,0:T(8,128)} all-to-all(f32[16,256,128]{2,1,0:T(8,128)} %bitcast.13), channel_id=1, replica_groups=mesh['band'=16,'grid'=16] {'grid'}, dimensions={0} | all-to-all | bytes 4194304 | tf_op jit(solution)/shard_map/all_to_all | solution.py:221
  166.9 4.0 %final.1 = (f32[2,1,8,128,128]{4,3,2,1,0:T(8,128)}, f32[2,1,8,128,128]{4,3,2,1,0:T(8,128)}) custom-call(f32[16,256,128]{2,1,0:T(8,128)} %all_to_all.25.pieces_ref, bf16[2,256,256]{2,1,0:T(8,128)(2,1)} %constant.121.clone.x_ref), custom_call_target="tpu_custom_call" | custom-call | tf_op jit(solution)/shard_map/final/pallas_call | solution.py:288
  (8 shorter events, 0.0 us)
Async XLA Ops:
  0.6 77.3 %copy-start = (f32[8,128,128]{2,1,0:T(8,128)S(1)}, f32[8,128,128]{2,1,0:T(8,128)}, u32[]{:S(2)}) copy-start(f32[8,128,128]{2,1,0:T(8,128)} %param.16) | copy-start | bytes 1572868
  4.1 35.5 %all-to-all-start = ((f32[16,128,128]{2,1,0:T(8,128)}), f32[16,128,128]{2,1,0:T(8,128)S(1)}, u32[]{:S(2)}, u32[]{:S(2)}) async-start(f32[16,128,128]{2,1,0:T(8,128)} %bitcast.15), calls=%async_computation | async-start | bytes 2097152 | tf_op jit(solution)/shard_map/all_to_all | solution.py:221
  39.6 1.0 copy-start.2
  42.8 25.4 %all-to-all-start.1 = ((f32[256,1,128]{2,1,0:T(1,128)}), f32[256,1,128]{2,1,0:T(1,128)S(1)}, u32[]{:S(2)}, u32[]{:S(2)}) async-start(f32[256,1,128]{2,1,0:T(1,128)} %bitcast.19), calls=%async_computation.1 | async-start | bytes 262144 | tf_op jit(solution)/shard_map/all_to_all | solution.py:221
  68.2 0.7 copy-start.3
  72.5 18.7 %all-to-all-start.2 = ((f32[256,1,128]{2,1,0:T(1,128)}), f32[256,1,128]{2,1,0:T(1,128)S(1)}, u32[]{:S(2)}, u32[]{:S(2)}) async-start(f32[256,1,128]{2,1,0:T(1,128)} %bitcast.17), calls=%async_computation.2 | async-start | bytes 262144 | tf_op jit(solution)/shard_map/all_to_all | solution.py:221
  91.2 0.7 copy-start.4
  94.1 29.5 %all-to-all-start.3 = ((f32[16,128,128]{2,1,0:T(8,128)}), f32[16,128,128]{2,1,0:T(8,128)S(1)}, u32[]{:S(2)}, u32[]{:S(2)}) async-start(f32[16,128,128]{2,1,0:T(8,128)} %share_back.1), calls=%async_computation.3 | async-start | bytes 2097152 | tf_op jit(solution)/shard_map/all_to_all | solution.py:221
  123.6 1.0 copy-start.1

commit v2 on v1

v2 whole, which is shorter than its diff:
```python
import functools
import math

import jax
import jax.numpy as jnp
import numpy as np
from jax import lax
from jax.experimental import pallas as pl
from jax.experimental.pallas import tpu as pltpu
from jax.sharding import PartitionSpec as P

box_length = 30.0
NARROW = jnp.bfloat16
WIDE = jnp.float32
ROWS = 2
GRANT = 20 * 2**20


def halves(table):
    high = table.astype(np.float32).astype(jnp.bfloat16)
    low = (table - high.astype(np.float64)).astype(np.float32).astype(jnp.bfloat16)
    return np.stack([high, low])


@functools.cache
def make_tables(length):
    wrapped = np.outer(np.arange(length), np.arange(length)) % length
    angles = wrapped.astype(np.float64) * (2.0 * math.pi / length)
    cosine, sine = np.cos(angles), np.sin(angles)
    return {
        "down": halves(np.block([[cosine, sine], [-sine, cosine]])),
        "up": halves(np.block([[cosine, -sine], [sine, cosine]])),
        "last": halves(np.block([[cosine, -sine], [sine, cosine]]) * float(length) ** -1.5),
    }


def split(value):
    high = value.astype(NARROW)
    return high, (value - high.astype(WIDE)).astype(NARROW)


def mul(left, right):
    return lax.dot_general(left, right, (((1,), (0,)), ((), ())), preferred_element_type=WIDE)


def product(left, right):
    left_high, left_low = left
    right_high, right_low = right
    return mul(left_high, right_high) + mul(left_low, right_high) + mul(left_high, right_low)


def pair(ref):
    return ref[0], ref[1]


def swap_blocks(value):
    rows, columns = value.shape[0] // 2, value.shape[1] // 2
    left = jnp.concatenate([value[:rows, :columns], value[rows:, :columns]], axis=1)
    right = jnp.concatenate([value[:rows, columns:], value[rows:, columns:]], axis=1)
    return jnp.concatenate([left, right], axis=0)


def parts_down(value):
    half = value.shape[1] // 2
    return jnp.concatenate([value[:, :half], value[:, half:]], axis=0)


def parts_across(value):
    half = value.shape[0] // 2
    return jnp.concatenate([value[:half], value[half:]], axis=1)


def density_kernel(orbital_ref, trial_ref, up_ref, down_ref, out_ref):
    length = orbital_ref.shape[2]
    parts, share = out_ref.shape[0], out_ref.shape[3]
    rows = orbital_ref.shape[1]
    values = []
    for x in range(rows):
        orbital = 2.0 * orbital_ref[0, x].astype(WIDE)
        values.append(
            jnp.concatenate([trial_ref[k, 0, x].astype(WIDE) * orbital for k in range(2)], axis=1)
        )
    turned = product(split(jnp.concatenate(values, axis=0)), pair(up_ref))
    columns = [parts_down(turned[x * length : (x + 1) * length]) for x in range(rows)]
    turned = product(pair(down_ref), split(jnp.concatenate(columns, axis=1)))
    for x in range(rows):
        for part in range(2):
            block = turned[part * length : (part + 1) * length, x * length : (x + 1) * length]
            out_ref[:, part, x] = block.reshape(parts, share, length)


def share_kernel(pieces_ref, share_ref, out_ref):
    total = pieces_ref[0]
    for i in range(1, pieces_ref.shape[0]):
        total = total + pieces_ref[i]
    share_ref[...] = total
    copies, rows, _ = out_ref.shape
    share = rows // 2
    for b in range(share):
        block = share_ref[pl.ds(b, rows, stride=share), :]
        for i in range(copies // share):
            out_ref[b * (copies // share) + i] = block


def line_kernel(pieces_ref, kernel_ref, down_ref, up_ref, out_ref):
    parts, rows, length = pieces_ref.shape
    share = rows // 2
    columns = jnp.concatenate(
        [pieces_ref[:, :share, :].reshape(length, length), pieces_ref[:, share:, :].reshape(length, length)],
        axis=0,
    )
    turned = product(pair(down_ref), split(columns))
    kernel = kernel_ref[...]
    turned = turned * jnp.concatenate([kernel, kernel], axis=0)
    out_ref[...] = product(pair(up_ref), split(turned)).reshape(parts, share, length)


def spread_kernel(pieces_ref, out_ref):
    share = pieces_ref.shape[0] // out_ref.shape[0]
    for part in range(2):
        for x in range(share):
            block = pieces_ref[pl.ds(part * share + x, share, stride=2 * share), :]
            rows = pl.ds((part * share + x) * share, share)
            for i in range(out_ref.shape[0]):
                out_ref[i, rows, :] = block


def back(blocks, up_ref, down_ref, length):
    turned = product(pair(up_ref), split(blocks))
    rows = turned.shape[1] // length
    points = [parts_across(turned[:, x * length : (x + 1) * length]) for x in range(rows)]
    return product(split(jnp.concatenate(points, axis=0)), pair(down_ref))


def reverse_bits(value, count):
    out = 0
    for i in range(count):
        out = out + (((value >> i) & 1) << (count - 1 - i))
    return out


def base_kernel(
    me_ref, energy_ref, near_ref, far_ref, orbital_ref, trial_ref, alda_ref, local_ref,
    up_ref, down_ref, out_ref,
):
    length = orbital_ref.shape[2]
    parts = 2 * near_ref.shape[0]
    share = length // parts
    bits = parts.bit_length() - 1
    me = me_ref[0]
    energy = energy_ref[0]
    even = (me & 1) == 0
    scale = 1.0 / float(length * length)
    rows = orbital_ref.shape[1]
    columns = []
    for x in range(rows):
        tiles = []
        for part in range(2):
            for half in range(parts // 2):
                slot = reverse_bits((half ^ (me >> 1)) << 1, bits)
                near = near_ref[slot, part, x]
                far = far_ref[slot, part, x]
                tiles.append(jnp.where(even, near, far))
                tiles.append(jnp.where(even, far, near))
        columns.append(jnp.concatenate(tiles, axis=0))
    value = back(jnp.concatenate(columns, axis=1), up_ref, down_ref, length)
    for x in range(rows):
        factor = orbital_ref[0, x].astype(WIDE) * (alda_ref[x] * scale)
        weight = local_ref[x] - energy
        for k in range(2):
            block = value[x * length : (x + 1) * length, k * length : (k + 1) * length]
            out_ref[k, x] = block * factor + weight * trial_ref[k, 0, x].astype(WIDE)


def field_kernel(potential_ref, orbital_ref, base_ref, up_ref, down_ref, out_ref):
    length = orbital_ref.shape[2]
    parts = potential_ref.shape[0]
    rows = orbital_ref.shape[1]
    columns = []
    for x in range(rows):
        columns.append(
            jnp.concatenate(
                [potential_ref[:, part, x].reshape(length, length) for part in range(2)], axis=0
            )
        )
    value = back(jnp.concatenate(columns, axis=1), up_ref, down_ref, length)
    fields = []
    for x in range(rows):
        orbital = orbital_ref[0, x].astype(WIDE)
        for k in range(2):
            block = value[x * length : (x + 1) * length, k * length : (k + 1) * length]
            fields.append(block * orbital + base_ref[k, x])
    table = (up_ref[0, :length, :], up_ref[1, :length, :])
    turned = product(split(jnp.concatenate(fields, axis=0)), table)
    for x in range(rows):
        points = swap_blocks(turned[2 * x * length : 2 * (x + 1) * length])
        waves = product(pair(down_ref), split(points))
        for k in range(2):
            for part in range(2):
                block = waves[part * length : (part + 1) * length, k * length : (k + 1) * length]
                out_ref[:, k, part, x] = block.reshape(parts, length // parts, length)


def final_kernel(pieces_ref, x_ref, real_ref, imag_ref):
    length = real_ref.shape[-1]
    share = real_ref.shape[2]
    table = pair(x_ref)
    for k in range(2):
        for b in range(share):
            parts = []
            for part in range(2):
                start = (k * 2 + part) * share * share + b
                block = pieces_ref[:, pl.ds(start, share, stride=share), :]
                parts.append(block.reshape(length, length))
            turned = product(split(jnp.concatenate(parts, axis=0).T), table)
            real_ref[k, 0, b] = turned[:, :length]
            imag_ref[k, 0, b] = turned[:, length:]


def signed(positions, length):
    return jnp.where(2 * positions < length, positions, positions - length).astype(WIDE)


def line_coulomb(b, length):
    a = lax.broadcasted_iota(jnp.int32, (length, length), 0)
    c = lax.broadcasted_iota(jnp.int32, (length, length), 1)
    squared = signed(a, length) ** 2 + signed(b, length) ** 2 + signed(c, length) ** 2
    scaled = box_length**2 / math.pi / jnp.maximum(squared, 1.0)
    return jnp.where(squared > 0, scaled, 0.0) / float(length**3)


def call(body, shapes, name, **options):
    return pl.pallas_call(
        body,
        out_shape=jax.tree.map(
            lambda s: jax.ShapeDtypeStruct(s, WIDE),
            shapes,
            is_leaf=lambda s: isinstance(s, tuple) and isinstance(s[0], int),
        ),
        name=name,
        compiler_params=pltpu.CompilerParams(vmem_limit_bytes=GRANT),
        **options,
    )


def exchange(array, axes):
    return lax.all_to_all(array, axes, split_axis=0, concat_axis=0, tiled=True)


def partner(array, axis, mask):
    return lax.ppermute(array, axis, [(i, i ^ mask) for i in range(lax.axis_size(axis))])


def per_device(orbitals, trials, alda_kernel, local_potential, band_energies):
    length = orbitals.shape[2]
    parts = lax.axis_size("band")
    share = length // parts
    points = share * share
    tables = {name: jnp.asarray(table) for name, table in make_tables(length).items()}
    me = lax.axis_index("band")
    place = lax.axis_index("grid")
    copies = parts // share
    kernel = line_coulomb(me * share + place // copies, length)
    own_up = lax.dynamic_slice_in_dim(tables["up"], (place % copies) * length, length, 1)

    scalar = pl.BlockSpec(memory_space=pltpu.SMEM)
    orbital_block = pl.BlockSpec((1, ROWS, length, length), lambda i: (0, i, 0, 0))
    trial_block = pl.BlockSpec((2, 1, ROWS, length, length), lambda i: (0, 0, i, 0, 0))
    table_block = pl.BlockSpec((2, 2 * length, 2 * length), lambda i: (0, 0, 0))
    share_block = pl.BlockSpec((parts, 2, ROWS, share, length), lambda i: (0, 0, i, 0, 0))
    half_block = pl.BlockSpec((parts // 2, 2, ROWS, share, length), lambda i: (0, 0, i, 0, 0))
    local_block = pl.BlockSpec((ROWS, length, length), lambda i: (i, 0, 0))
    base_block = pl.BlockSpec((2, ROWS, length, length), lambda i: (0, i, 0, 0))
    steps = (share // ROWS,)

    pieces = call(
        density_kernel,
        (parts, 2, share, share, length),
        "density",
        grid=steps,
        in_specs=[orbital_block, trial_block, table_block, table_block],
        out_specs=share_block,
    )(orbitals, trials, tables["up"], tables["down"])
    pieces = exchange(pieces.reshape(parts, 2 * points, length), "band")
    spectrum, lines = call(
        share_kernel, [(2 * points, length), (parts, 2 * share, length)], "share"
    )(pieces)
    masks = [parts >> (i + 1) for i in range(parts.bit_length() - 1)]
    held = spectrum[None]
    far = partner(held, "band", masks[0])
    lines, far = lax.optimization_barrier((exchange(lines, "grid"), far))
    held = jnp.concatenate([held, far], axis=0)
    far = partner(held, "band", masks[1])
    lines = call(line_kernel, (parts, share, length), "line")(
        lines, kernel, tables["down"], own_up
    )
    lines, far = lax.optimization_barrier((exchange(lines, "grid"), far))
    lines = lines.reshape(parts * share, length)
    for mask in masks[2:]:
        held = jnp.concatenate([held, far], axis=0)
        far = partner(held, "band", mask)
    potential = call(spread_kernel, (parts, 2 * points, length), "spread")(lines)
    potential = exchange(potential, "band").reshape(parts, 2, share, share, length)
    base = call(
        base_kernel,
        (2, share, length, length),
        "base",
        grid=steps,
        in_specs=[
            scalar, scalar, half_block, half_block, orbital_block, trial_block,
            local_block, local_block, table_block, table_block,
        ],
        out_specs=base_block,
    )(
        me.reshape(1),
        band_energies,
        held.reshape(parts // 2, 2, share, share, length),
        far.reshape(parts // 2, 2, share, share, length),
        orbitals,
        trials,
        alda_kernel,
        local_potential,
        tables["up"],
        tables["down"],
    )
    fields = call(
        field_kernel,
        (parts, 2, 2, share, share, length),
        "field",
        grid=steps,
        in_specs=[share_block, orbital_block, base_block, table_block, table_block],
        out_specs=pl.BlockSpec(
            (parts, 2, 2, ROWS, share, length), lambda i: (0, 0, 0, i, 0, 0)
        ),
    )(potential, orbitals, base, tables["up"], tables["down"])
    received = exchange(fields.reshape(parts, 4 * points, length), "grid")
    shape = (2, 1, share, length, length)
    return tuple(call(final_kernel, [shape, shape], "final")(received, tables["last"]))


def solution(mesh):
    placed = (
        P("band", "grid", None, None),
        P(None, "band", "grid", None, None),
        P("grid", None, None),
        P("grid", None, None),
        P("band"),
    )
    return jax.shard_map(
        per_device,
        mesh=mesh,
        in_specs=placed,
        out_specs=(P(None, "band", "grid", None, None), P(None, "band", "grid", None, None)),
        check_vma=False,
    )
```

time: 171 us -> 173 us (1.012)
  blocking collectives: 36.3 us -> 47.9 us
  waiting for transfers between devices: 75.2 us -> 70.7 us
  Pallas kernels: 21.6 us -> 17.8 us
    all_to_all x4 -> x3, waiting for transfers between devices: 75.2 us -> 25.4 us  [exchange(): return lax.all_to_all(array, axes, split_axis=0, concat_axis=0, tiled=True)]
    ppermute x0 -> x4, waiting for transfers between devices: none -> 45.3 us  [partner(): lax.ppermute(array, axis, [(i, i ^ mask) for i in range(lax.axis_size(axi...]
    all_to_all x1 -> x2, blocking collectives: 36.3 us -> 47.9 us  [exchange(): return lax.all_to_all(array, axes, split_axis=0, concat_axis=0, tiled=True)]
    all_to_all x4 -> x3, starting transfers between devices: 31.5 us -> 26.7 us  [exchange(): return lax.all_to_all(array, axes, split_axis=0, concat_axis=0, tiled=True)]
    ppermute x0 -> x4, starting transfers between devices: none -> 3.89 us  [partner(): lax.ppermute(array, axis, [(i, i ^ mask) for i in range(lax.axis_size(axi...]
    pallas_call x6 -> x7, Pallas kernels: 21.6 us -> 17.8 us  [the longest x1 6.61 us: per_device(): call(field_kernel, (parts, 2, 2, share, share, length), 'field', grid=ste...]
    unnamed x10 -> x22, local copies, waits for them, and re-layouts: 3.26 us -> 3.92 us
  transfers between devices with their start and end apart: 4 -> 7, of which waited for: 4 -> 4; matrix products, arithmetic and copies ran while one was open for 1% -> 0% of each run, Pallas kernels for 0% -> 2%
where the time goes in v2:
time: 173 us
  waiting for transfers between devices  70.7 us (41%)
  blocking collectives  47.9 us (28%)
  starting transfers between devices  30.6 us (18%)
  Pallas kernels  17.8 us (10%)
  local copies, waits for them, and re-layouts  3.94 us (2%)
    all_to_all x2, blocking collectives, exchange(): return lax.all_to_all(array, axes, split_axis=0, concat_axis=0, tiled=True)  47.9 us
    ppermute x4, waiting for transfers between devices, partner(): lax.ppermute(array, axis, [(i, i ^ mask) for i in range(lax.axis_size(axi...  45.3 us
    all_to_all x3, starting transfers between devices, exchange(): return lax.all_to_all(array, axes, split_axis=0, concat_axis=0, tiled=True)  26.7 us
    all_to_all x3, waiting for transfers between devices, exchange(): return lax.all_to_all(array, axes, split_axis=0, concat_axis=0, tiled=True)  25.4 us
    pallas_call x1, Pallas kernels, per_device(): call(field_kernel, (parts, 2, 2, share, share, length), 'field', grid=ste...  6.61 us
    unnamed x22, local copies, waits for them, and re-layouts  3.92 us
    ppermute x4, starting transfers between devices, partner(): lax.ppermute(array, axis, [(i, i ^ mask) for i in range(lax.axis_size(axi...  3.89 us
    pallas_call x1, Pallas kernels, per_device(): call(density_kernel, (parts, 2, share, share, length), 'density', grid=st...  3.54 us
  transfers between devices with their start and end apart: 7, of which 4 were waited for; matrix products, arithmetic and copies ran while one was open for 0% of the time, Pallas kernels for 2%

profile of v2, /device:TPU:1, one launch (start us, length us, event | category | flops | bytes accessed | tf_op | source)
XLA Modules:
  0.0 172.7 jit_solution(10668494390118301163)
XLA Ops:
  0.6 0.9 copy-done
  1.6 0.9 copy-done.2
  2.5 0.9 copy-done.4
  3.5 1.0 copy-done.6
  4.5 3.5 %density.1 = f32[16,2,8,8,128]{4,3,2,1,0:T(8,128)} custom-call(bf16[1,8,128,128]{3,2,1,0:T(8,128)(2,1)S(1)} %copy-done.4, bf16[2,1,8,128,128]{4,3,2,1,0:T(8,128)(2,1)S(1)} %copy-done.6, bf16[2,256,256]{2,1,0:T(8,128)(2,1)S(1)} %copy-done.2, bf16[2,256,256]{2,1,0:T(8,128)(2,1)S(1)} %copy-done), custom_call_target="tpu_custom_call" | custom-call | tf_op jit(solution)/shard_map/density/pallas_call | solution.py:276
  8.1 10.2 %all-to-all-start = ((f32[16,128,128]{2,1,0:T(8,128)}), f32[16,128,128]{2,1,0:T(8,128)S(1)}, u32[]{:S(2)}, u32[]{:S(2)}) async-start(f32[16,128,128]{2,1,0:T(8,128)} %bitcast), calls=%async_computation | async-start | bytes 2097152 | tf_op jit(solution)/shard_map/all_to_all | solution.py:247
  18.4 25.4 %all-to-all-done.pieces_ref = f32[16,128,128]{2,1,0:T(8,128)S(1)} async-done(((f32[16,128,128]{2,1,0:T(8,128)}), f32[16,128,128]{2,1,0:T(8,128)S(1)}, u32[]{:S(2)}, u32[]{:S(2)}) %all-to-all-start) | async-done | bytes 1048608 | tf_op jit(solution)/shard_map/all_to_all | solution.py:247
  43.8 0.7 share.1
  44.5 10.9 %all-to-all-start.1 = ((f32[16,16,128]{2,1,0:T(8,128)}), f32[16,16,128]{2,1,0:T(8,128)S(1)}, u32[]{:S(2)}, u32[]{:S(2)}) async-start(f32[16,16,128]{2,1,0:T(8,128)} %get-tuple-element.8), calls=%async_computation.1 | async-start | bytes 262144 | tf_op jit(solution)/shard_map/all_to_all | solution.py:247
  55.4 1.1 collective-permute-start
  56.5 0.1 select_multiply_fusion.kernel_ref
  56.6 6.7 %collective-permute-done = f32[1,128,128]{2,1,0:T(8,128)S(1)} collective-permute-done((f32[1,128,128]{2,1,0:T(8,128)S(1)}, f32[1,128,128]{2,1,0:T(8,128)S(1)}, u32[]{:S(2)}, u32[]{:S(2)}) %collective-permute-start) | collective-permute-done | bytes 65568 | tf_op jit(solution)/shard_map/ppermute | solution.py:251
  63.5 0.5 line.1
  63.9 15.0 %all_to_all.25 = f32[16,8,128]{2,1,0:T(8,128)S(1)} all-to-all(f32[16,8,128]{2,1,0:T(8,128)S(1)} %line.1), channel_id=1, replica_groups=mesh['band'=16,'grid'=16] {'grid'}, dimensions={0} | all-to-all | bytes 131072 | tf_op jit(solution)/shard_map/all_to_all | solution.py:247
  78.9 1.1 spread.1
  80.0 5.5 %all-to-all-start.3 = ((f32[16,128,128]{2,1,0:T(8,128)}), f32[16,128,128]{2,1,0:T(8,128)S(1)}, u32[]{:S(2)}, u32[]{:S(2)}) async-start(f32[16,128,128]{2,1,0:T(8,128)} %spread.1), calls=%async_computation.3 | async-start | bytes 2097152 | tf_op jit(solution)/shard_map/all_to_all | solution.py:247
  85.6 1.4 collective-permute-start.2
  87.0 28.4 %collective-permute-done.2 = f32[4,128,128]{2,1,0:T(8,128)S(1)} collective-permute-done((f32[4,128,128]{2,1,0:T(8,128)S(1)}, f32[4,128,128]{2,1,0:T(8,128)S(1)}, u32[]{:S(2)}, u32[]{:S(2)}) %collective-permute-start.2) | collective-permute-done | bytes 262176 | tf_op jit(solution)/shard_map/ppermute | solution.py:251
  115.5 1.3 collective-permute-start.3
  117.5 10.2 %collective-permute-done.3 = f32[8,128,128]{2,1,0:T(8,128)S(1)} collective-permute-done((f32[8,128,128]{2,1,0:T(8,128)S(1)}, f32[8,128,128]{2,1,0:T(8,128)S(1)}, u32[]{:S(2)}, u32[]{:S(2)}) %collective-permute-start.3) | collective-permute-done | bytes 524320 | tf_op jit(solution)/shard_map/ppermute | solution.py:251
  127.7 3.0 %base.1.base_ref = f32[2,8,128,128]{3,2,1,0:T(8,128)S(1)} custom-call(s32[1]{0:T(128)} %bitcast.4.me_ref, f32[1]{0:T(128)S(6)} %copy.10.energy_ref, f32[8,2,8,8,128]{4,3,2,1,0:T(8,128)S(1)} %pad_maximum_fusion.near_ref, f32[8,2,8,8,128]{4,3,2,1,0:T(8,128)S(1)} %bitcast.18, bf16[1,8,128,128]{3,2,1,0:T(8,128)(2,1)S(1)} %copy-done.5, ...), custom_call_target="tpu_custom_call" | custom-call | tf_op jit(solution)/shard_map/base/pallas_call | solution.py:304
  130.7 6.6 %field.1 = f32[16,2,2,8,8,128]{5,4,3,2,1,0:T(8,128)S(1)} custom-call(f32[16,2,8,8,128]{4,3,2,1,0:T(8,128)S(1)} %bitcast.12, bf16[1,8,128,128]{3,2,1,0:T(8,128)(2,1)S(1)} %copy-done.5, f32[2,8,128,128]{3,2,1,0:T(8,128)S(1)} %base.1.base_ref, bf16[2,256,256]{2,1,0:T(8,128)(2,1)S(1)} %copy-done.3, bf16[2,256,256]{2,1,0:T(8,128)(2,1)S(1)} %copy-done.1), custom_call_target="tpu_custom_call" | custom-call | tf_op jit(solution)/shard_map/field/pallas_call | solution.py:326
  137.4 33.0 %all_to_all.26.pieces_ref = f32[16,256,128]{2,1,0:T(8,128)S(1)} all-to-all(f32[16,256,128]{2,1,0:T(8,128)S(1)} %bitcast.11), channel_id=1, replica_groups=mesh['band'=16,'grid'=16] {'grid'}, dimensions={0} | all-to-all | bytes 4194304 | tf_op jit(solution)/shard_map/all_to_all | solution.py:247
  170.3 2.4 %final.1 = (f32[2,1,8,128,128]{4,3,2,1,0:T(8,128)}, f32[2,1,8,128,128]{4,3,2,1,0:T(8,128)}) custom-call(f32[16,256,128]{2,1,0:T(8,128)S(1)} %all_to_all.26.pieces_ref, bf16[2,256,256]{2,1,0:T(8,128)(2,1)S(1)} %copy-done.10), custom_call_target="tpu_custom_call" | custom-call | tf_op jit(solution)/shard_map/final/pallas_call | solution.py:338
  (29 shorter events, 0.3 us)
Async XLA Ops:
  0.6 1.0 copy-start
  1.6 0.9 copy-start.2
  2.5 0.9 copy-start.4
  3.5 1.0 copy-start.6
  8.1 55.3 %copy-start.3 = (bf16[2,256,256]{2,1,0:T(8,128)(2,1)S(1)}, bf16[2,256,256]{2,1,0:T(8,128)(2,1)}, u32[]{:S(2)}) copy-start(bf16[2,256,256]{2,1,0:T(8,128)(2,1)} %constant.61.clone.up_ref) | copy-start | bytes 786436
  8.1 55.4 %copy-start.1 = (bf16[2,256,256]{2,1,0:T(8,128)(2,1)S(1)}, bf16[2,256,256]{2,1,0:T(8,128)(2,1)}, u32[]{:S(2)}) copy-start(bf16[2,256,256]{2,1,0:T(8,128)(2,1)} %constant.60.clone.down_ref) | copy-start | bytes 786436
  8.1 35.7 %all-to-all-start = ((f32[16,128,128]{2,1,0:T(8,128)}), f32[16,128,128]{2,1,0:T(8,128)S(1)}, u32[]{:S(2)}, u32[]{:S(2)}) async-start(f32[16,128,128]{2,1,0:T(8,128)} %bitcast), calls=%async_computation | async-start | bytes 2097152 | tf_op jit(solution)/shard_map/all_to_all | solution.py:247
  44.5 18.8 %all-to-all-start.1 = ((f32[16,16,128]{2,1,0:T(8,128)}), f32[16,16,128]{2,1,0:T(8,128)S(1)}, u32[]{:S(2)}, u32[]{:S(2)}) async-start(f32[16,16,128]{2,1,0:T(8,128)} %get-tuple-element.8), calls=%async_computation.1 | async-start | bytes 262144 | tf_op jit(solution)/shard_map/all_to_all | solution.py:247
  55.4 7.9 %collective-permute-start = (f32[1,128,128]{2,1,0:T(8,128)S(1)}, f32[1,128,128]{2,1,0:T(8,128)S(1)}, u32[]{:S(2)}, u32[]{:S(2)}) collective-permute-start(f32[1,128,128]{2,1,0:T(8,128)S(1)} %bitcast.13), channel_id=1, source_target_pairs={{0,128},{16,144},{32,160},{48,176},{64,192},{80,208},{96,224},{112... | collective-permute-start | bytes 196616 | tf_op jit(solution)/shard_map/ppermute | solution.py:251
  63.3 15.6 %collective-permute-start.1 = (f32[2,128,128]{2,1,0:T(8,128)S(1)}, f32[2,128,128]{2,1,0:T(8,128)S(1)}, u32[]{:S(2)}, u32[]{:S(2)}) collective-permute-start(f32[2,128,128]{2,1,0:T(8,128)S(1)} %pad_maximum_fusion.3), channel_id=1, source_target_pairs={{0,64},{16,80},{32,96},{48,112},{64,0},{80,16},{96,32},{112,48},{1... | collective-permute-start | bytes 393224 | tf_op jit(solution)/shard_map/ppermute | solution.py:251
  80.0 47.7 %copy-start.5 = (bf16[1,8,128,128]{3,2,1,0:T(8,128)(2,1)S(1)}, bf16[1,8,128,128]{3,2,1,0:T(8,128)(2,1)}, u32[]{:S(2)}) copy-start(bf16[1,8,128,128]{3,2,1,0:T(8,128)(2,1)} %orbital_ref.5) | copy-start | bytes 786436
  80.0 47.7 %copy-start.7 = (bf16[2,1,8,128,128]{4,3,2,1,0:T(8,128)(2,1)S(1)}, bf16[2,1,8,128,128]{4,3,2,1,0:T(8,128)(2,1)}, u32[]{:S(2)}) copy-start(bf16[2,1,8,128,128]{4,3,2,1,0:T(8,128)(2,1)} %trial_ref.3) | copy-start | bytes 1572868
  80.0 50.7 %all-to-all-start.3 = ((f32[16,128,128]{2,1,0:T(8,128)}), f32[16,128,128]{2,1,0:T(8,128)S(1)}, u32[]{:S(2)}, u32[]{:S(2)}) async-start(f32[16,128,128]{2,1,0:T(8,128)} %spread.1), calls=%async_computation.3 | async-start | bytes 2097152 | tf_op jit(solution)/shard_map/all_to_all | solution.py:247
  85.5 42.2 %copy-start.8 = (f32[8,128,128]{2,1,0:T(8,128)S(1)}, f32[8,128,128]{2,1,0:T(8,128)}, u32[]{:S(2)}) copy-start(f32[8,128,128]{2,1,0:T(8,128)} %alda_ref.1) | copy-start | bytes 1572868
  85.5 42.2 %copy-start.9 = (f32[8,128,128]{2,1,0:T(8,128)S(1)}, f32[8,128,128]{2,1,0:T(8,128)}, u32[]{:S(2)}) copy-start(f32[8,128,128]{2,1,0:T(8,128)} %local_ref.1) | copy-start | bytes 1572868
  85.6 29.9 %collective-permute-start.2 = (f32[4,128,128]{2,1,0:T(8,128)S(1)}, f32[4,128,128]{2,1,0:T(8,128)S(1)}, u32[]{:S(2)}, u32[]{:S(2)}) collective-permute-start(f32[4,128,128]{2,1,0:T(8,128)S(1)} %pad_maximum_fusion.2), channel_id=1, source_target_pairs={{0,32},{16,48},{32,0},{48,16},{64,96},{80,112},{96,64},{112,80},{1... | collective-permute-start | bytes 786440 | tf_op jit(solution)/shard_map/ppermute | solution.py:251
  115.5 12.2 %collective-permute-start.3 = (f32[8,128,128]{2,1,0:T(8,128)S(1)}, f32[8,128,128]{2,1,0:T(8,128)S(1)}, u32[]{:S(2)}, u32[]{:S(2)}) collective-permute-start(f32[8,128,128]{2,1,0:T(8,128)S(1)} %pad_maximum_fusion.1), channel_id=1, source_target_pairs={{0,16},{16,0},{32,48},{48,32},{64,80},{80,64},{96,112},{112,96},{1... | collective-permute-start | bytes 1572872 | tf_op jit(solution)/shard_map/ppermute | solution.py:251
  137.4 33.0 %copy-start.10 = (bf16[2,256,256]{2,1,0:T(8,128)(2,1)S(1)}, bf16[2,256,256]{2,1,0:T(8,128)(2,1)}, u32[]{:S(2)}) copy-start(bf16[2,256,256]{2,1,0:T(8,128)(2,1)} %constant.62.clone.x_ref) | copy-start | bytes 786436

commit v3 on v2

--- a/solution.py
+++ b/solution.py
@@ -9,11 +9,13 @@
 from jax.experimental.pallas import tpu as pltpu
 from jax.sharding import PartitionSpec as P
 
+
 box_length = 30.0
 NARROW = jnp.bfloat16
 WIDE = jnp.float32
 ROWS = 2
 GRANT = 20 * 2**20
+WIDE_GRANT = 60 * 2**20
 
 
 def halves(table):
@@ -132,21 +134,12 @@
     return product(split(jnp.concatenate(points, axis=0)), pair(down_ref))
 
 
-def reverse_bits(value, count):
-    out = 0
-    for i in range(count):
-        out = out + (((value >> i) & 1) << (count - 1 - i))
-    return out
-
-
 def base_kernel(
     me_ref, energy_ref, near_ref, far_ref, orbital_ref, trial_ref, alda_ref, local_ref,
     up_ref, down_ref, out_ref,
 ):
     length = orbital_ref.shape[2]
     parts = 2 * near_ref.shape[0]
-    share = length // parts
-    bits = parts.bit_length() - 1
     me = me_ref[0]
     energy = energy_ref[0]
     even = (me & 1) == 0
@@ -157,7 +150,7 @@
         tiles = []
         for part in range(2):
             for half in range(parts // 2):
-                slot = reverse_bits((half ^ (me >> 1)) << 1, bits)
+                slot = half ^ (me >> 1)
                 near = near_ref[slot, part, x]
                 far = far_ref[slot, part, x]
                 tiles.append(jnp.where(even, near, far))
@@ -229,7 +222,7 @@
     return jnp.where(squared > 0, scaled, 0.0) / float(length**3)
 
 
-def call(body, shapes, name, **options):
+def call(body, shapes, grant=GRANT, **options):
     return pl.pallas_call(
         body,
         out_shape=jax.tree.map(
@@ -237,18 +230,17 @@
             shapes,
             is_leaf=lambda s: isinstance(s, tuple) and isinstance(s[0], int),
         ),
-        name=name,
-        compiler_params=pltpu.CompilerParams(vmem_limit_bytes=GRANT),
+        compiler_params=pltpu.CompilerParams(vmem_limit_bytes=grant),
         **options,
     )
 
 
-def exchange(array, axes):
-    return lax.all_to_all(array, axes, split_axis=0, concat_axis=0, tiled=True)
-
-
-def partner(array, axis, mask):
-    return lax.ppermute(array, axis, [(i, i ^ mask) for i in range(lax.axis_size(axis))])
+def exchange(array, axis):
+    return lax.all_to_all(array, axis, split_axis=0, concat_axis=0, tiled=True)
+
+
+def partner(array, mask):
+    return lax.ppermute(array, "band", [(i, i ^ mask) for i in range(lax.axis_size("band"))])
 
 
 def per_device(orbitals, trials, alda_kernel, local_potential, band_energies):
@@ -276,35 +268,35 @@
     pieces = call(
         density_kernel,
         (parts, 2, share, share, length),
-        "density",
+        grant=WIDE_GRANT,
         grid=steps,
         in_specs=[orbital_block, trial_block, table_block, table_block],
         out_specs=share_block,
     )(orbitals, trials, tables["up"], tables["down"])
     pieces = exchange(pieces.reshape(parts, 2 * points, length), "band")
-    spectrum, lines = call(
-        share_kernel, [(2 * points, length), (parts, 2 * share, length)], "share"
-    )(pieces)
-    masks = [parts >> (i + 1) for i in range(parts.bit_length() - 1)]
-    held = spectrum[None]
-    far = partner(held, "band", masks[0])
-    lines, far = lax.optimization_barrier((exchange(lines, "grid"), far))
-    held = jnp.concatenate([held, far], axis=0)
-    far = partner(held, "band", masks[1])
-    lines = call(line_kernel, (parts, share, length), "line")(
+    spectrum, lines = call(share_kernel, [(2 * points, length), (parts, 2 * share, length)])(pieces)
+    lines = exchange(lines, "grid")
+    held = {0: spectrum}
+    for mask in (2, 4, 8):
+        held[mask] = partner(spectrum, mask)
+    lines, held[2], held[4], held[8] = lax.optimization_barrier((lines, held[2], held[4], held[8]))
+    lines = call(line_kernel, (parts, share, length))(
         lines, kernel, tables["down"], own_up
     )
-    lines, far = lax.optimization_barrier((exchange(lines, "grid"), far))
+    lines = exchange(lines, "grid")
+    both = partner(jnp.stack([held[4], held[8]]), 2)
+    held[6], held[10] = both[0], both[1]
+    held[12] = partner(held[8], 4)
+    held[14] = partner(spectrum, 14)
+    near = jnp.stack([held[mask] for mask in range(0, parts, 2)])
+    lines, near = lax.optimization_barrier((lines, near))
+    far = partner(near, 1)
     lines = lines.reshape(parts * share, length)
-    for mask in masks[2:]:
-        held = jnp.concatenate([held, far], axis=0)
-        far = partner(held, "band", mask)
-    potential = call(spread_kernel, (parts, 2 * points, length), "spread")(lines)
+    potential = call(spread_kernel, (parts, 2 * points, length))(lines)
     potential = exchange(potential, "band").reshape(parts, 2, share, share, length)
     base = call(
         base_kernel,
         (2, share, length, length),
-        "base",
         grid=steps,
         in_specs=[
             scalar, scalar, half_block, half_block, orbital_block, trial_block,
@@ -314,7 +306,7 @@
     )(
         me.reshape(1),
         band_energies,
-        held.reshape(parts // 2, 2, share, share, length),
+        near.reshape(parts // 2, 2, share, share, length),
         far.reshape(parts // 2, 2, share, share, length),
         orbitals,
         trials,
@@ -326,7 +318,6 @@
     fields = call(
         field_kernel,
         (parts, 2, 2, share, share, length),
-        "field",
         grid=steps,
         in_specs=[share_block, orbital_block, base_block, table_block, table_block],
         out_specs=pl.BlockSpec(
@@ -335,7 +326,7 @@
     )(potential, orbitals, base, tables["up"], tables["down"])
     received = exchange(fields.reshape(parts, 4 * points, length), "grid")
     shape = (2, 1, share, length, length)
-    return tuple(call(final_kernel, [shape, shape], "final")(received, tables["last"]))
+    return tuple(call(final_kernel, [shape, shape])(received, tables["last"]))
 
 
 def solution(mesh):
@@ -346,6 +337,7 @@
         P("grid", None, None),
         P("band"),
     )
+
     return jax.shard_map(
         per_device,
         mesh=mesh,

time: 173 us -> 159 us (0.919)
  waiting for transfers between devices: 70.7 us -> 55.9 us
  blocking collectives: 47.9 us -> 39.3 us
  starting transfers between devices: 30.6 us -> 38.3 us
  Pallas kernels: 17.8 us -> 19.8 us
    ppermute x4 -> x7, waiting for transfers between devices: 45.3 us -> 18.3 us  [partner(): lax.ppermute(array, 'band', [(i, i ^ mask) for i in range(lax.axis_size('...]
    all_to_all x3 -> x4, waiting for transfers between devices: 25.4 us -> 37.6 us  [exchange(): return lax.all_to_all(array, axis, split_axis=0, concat_axis=0, tiled=True)]
    all_to_all x2 -> x1, blocking collectives: 47.9 us -> 39.3 us  [exchange(): return lax.all_to_all(array, axis, split_axis=0, concat_axis=0, tiled=True)]
    ppermute x4 -> x7, starting transfers between devices: 3.89 us -> 10.3 us  [partner(): lax.ppermute(array, 'band', [(i, i ^ mask) for i in range(lax.axis_size('...]
    pallas_call x7, Pallas kernels: 17.8 us -> 19.8 us  [the longest x1 6.6 us: per_device(): call(field_kernel, (parts, 2, 2, share, share, length), grid=steps, in_sp...]
    all_to_all x3 -> x4, starting transfers between devices: 26.7 us -> 28 us  [exchange(): return lax.all_to_all(array, axis, split_axis=0, concat_axis=0, tiled=True)]
    unnamed x22 -> x25, local copies, waits for them, and re-layouts: 3.92 us -> 3.2 us
  transfers between devices with their start and end apart: 7 -> 11, of which waited for: 4 -> 6; matrix products, arithmetic and copies ran while one was open for 0% -> 0% of each run, Pallas kernels for 2% -> 3%
where the time goes in v3:
time: 159 us; the launch traced here: 158 us
  waiting for transfers between devices  55.9 us (35%)
  blocking collectives  39.3 us (25%)
  starting transfers between devices  38.3 us (24%)
  Pallas kernels  19.8 us (12%)
  local copies, waits for them, and re-layouts  3.22 us (2%)
    all_to_all x1, blocking collectives, exchange(): return lax.all_to_all(array, axis, split_axis=0, concat_axis=0, tiled=True)  39.3 us
    all_to_all x4, waiting for transfers between devices, exchange(): return lax.all_to_all(array, axis, split_axis=0, concat_axis=0, tiled=True)  37.6 us
    all_to_all x4, starting transfers between devices, exchange(): return lax.all_to_all(array, axis, split_axis=0, concat_axis=0, tiled=True)  28 us
    ppermute x7, waiting for transfers between devices, partner(): lax.ppermute(array, 'band', [(i, i ^ mask) for i in range(lax.axis_size('...  18.3 us
    ppermute x7, starting transfers between devices, partner(): lax.ppermute(array, 'band', [(i, i ^ mask) for i in range(lax.axis_size('...  10.3 us
    pallas_call x1, Pallas kernels, per_device(): call(field_kernel, (parts, 2, 2, share, share, length), grid=steps, in_sp...  6.6 us
    pallas_call x1, Pallas kernels, per_device(): call(density_kernel, (parts, 2, share, share, length), grant=WIDE_GRANT,...  5.05 us
    unnamed x25, local copies, waits for them, and re-layouts  3.2 us
  transfers between devices with their start and end apart: 11, of which 6 were waited for; matrix products, arithmetic and copies ran while one was open for 0% of the time, Pallas kernels for 3%

profile of v3, /device:TPU:1, one launch (start us, length us, event | category | flops | bytes accessed | tf_op | source)
XLA Modules:
  0.0 158.2 jit_solution(16194673045070103595)
XLA Ops:
  0.6 5.1 %shard_map.95 = f32[16,2,8,8,128]{4,3,2,1,0:T(8,128)} custom-call(bf16[1,8,128,128]{3,2,1,0:T(8,128)(2,1)} %orbital_ref.5, bf16[2,1,8,128,128]{4,3,2,1,0:T(8,128)(2,1)} %trial_ref.3, bf16[2,256,256]{2,1,0:T(8,128)(2,1)} %constant.61.clone.up_ref, bf16[2,256,256]{2,1,0:T(8,128)(2,1)} %constant.60.clone.down_ref), custom_call_target="tpu_custom_call" | custom-call | tf_op jit(solution)/shard_map/pallas_call | solution.py:268
  5.7 10.3 %all-to-all-start = ((f32[16,128,128]{2,1,0:T(8,128)}), f32[16,128,128]{2,1,0:T(8,128)S(1)}, u32[]{:S(2)}, u32[]{:S(2)}) async-start(f32[16,128,128]{2,1,0:T(8,128)} %bitcast.24), calls=%async_computation | async-start | bytes 2097152 | tf_op jit(solution)/shard_map/all_to_all | solution.py:239
  16.2 25.2 %all-to-all-done.pieces_ref = f32[16,128,128]{2,1,0:T(8,128)S(1)} async-done(((f32[16,128,128]{2,1,0:T(8,128)}), f32[16,128,128]{2,1,0:T(8,128)S(1)}, u32[]{:S(2)}, u32[]{:S(2)}) %all-to-all-start) | async-done | bytes 1048608 | tf_op jit(solution)/shard_map/all_to_all | solution.py:239
  41.4 0.7 shard_map.96
  42.1 1.1 collective-permute-start.5
  43.2 6.1 %collective-permute-start.2 = (f32[128,128]{1,0:T(8,128)S(1)}, f32[128,128]{1,0:T(8,128)S(1)}, u32[]{:S(2)}, u32[]{:S(2)}) collective-permute-start(f32[128,128]{1,0:T(8,128)S(1)} %get-tuple-element.11), channel_id=1, source_target_pairs={{0,128},{16,144},{32,160},{48,176},{64,192},{80,208},{96,224},{112... | collective-permute-start | bytes 196616 | tf_op jit(solution)/shard_map/ppermute | solution.py:243
  49.7 10.4 %all-to-all-start.1 = ((f32[16,16,128]{2,1,0:T(8,128)}), f32[16,16,128]{2,1,0:T(8,128)S(1)}, u32[]{:S(2)}, u32[]{:S(2)}) async-start(f32[16,16,128]{2,1,0:T(8,128)} %get-tuple-element.10), calls=%async_computation.1 | async-start | bytes 262144 | tf_op jit(solution)/shard_map/all_to_all | solution.py:239
  60.1 7.6 %all-to-all-done.1.pieces_ref = f32[16,16,128]{2,1,0:T(8,128)S(1)} async-done(((f32[16,16,128]{2,1,0:T(8,128)}), f32[16,16,128]{2,1,0:T(8,128)S(1)}, u32[]{:S(2)}, u32[]{:S(2)}) %all-to-all-start.1) | async-done | bytes 131104 | tf_op jit(solution)/shard_map/all_to_all | solution.py:239
  67.7 1.1 shard_map.97
  68.8 3.7 %all-to-all-start.2 = ((f32[16,8,128]{2,1,0:T(8,128)}), f32[16,8,128]{2,1,0:T(8,128)S(1)}, u32[]{:S(2)}, u32[]{:S(2)}) async-start(f32[16,8,128]{2,1,0:T(8,128)} %shard_map.97), calls=%async_computation.2 | async-start | bytes 131072 | tf_op jit(solution)/shard_map/all_to_all | solution.py:239
  72.6 1.0 collective-permute-start.4
  74.1 5.7 %collective-permute-done.3 = f32[2,128,128]{2,1,0:T(8,128)S(1)} collective-permute-done((f32[2,128,128]{2,1,0:T(8,128)S(1)}, f32[2,128,128]{2,1,0:T(8,128)S(1)}, u32[]{:S(2)}, u32[]{:S(2)}) %collective-permute-start.3) | collective-permute-done | bytes 131104 | tf_op jit(solution)/shard_map/ppermute | solution.py:243
  80.0 1.1 shard_map.98
  81.1 3.7 %all-to-all-start.3 = ((f32[16,128,128]{2,1,0:T(8,128)}), f32[16,128,128]{2,1,0:T(8,128)S(1)}, u32[]{:S(2)}, u32[]{:S(2)}) async-start(f32[16,128,128]{2,1,0:T(8,128)} %shard_map.98), calls=%async_computation.3 | async-start | bytes 2097152 | tf_op jit(solution)/shard_map/all_to_all | solution.py:239
  84.7 1.3 collective-permute-start.6
  86.6 12.6 %collective-permute-done.6 = f32[8,128,128]{2,1,0:T(8,128)S(1)} collective-permute-done((f32[8,128,128]{2,1,0:T(8,128)S(1)}, f32[8,128,128]{2,1,0:T(8,128)S(1)}, u32[]{:S(2)}, u32[]{:S(2)}) %collective-permute-start.6) | collective-permute-done | bytes 524320 | tf_op jit(solution)/shard_map/ppermute | solution.py:243
  99.3 1.0 copy-done.5
  100.3 1.0 copy-done.6
  101.4 1.0 copy-done.7
  102.4 2.9 %shard_map.99.base_ref = f32[2,8,128,128]{3,2,1,0:T(8,128)S(1)} custom-call(s32[1]{0:T(128)} %bitcast.9.me_ref, f32[1]{0:T(128)S(6)} %copy.17.energy_ref, f32[8,2,8,8,128]{4,3,2,1,0:T(8,128)S(1)} %bitcast.21, f32[8,2,8,8,128]{4,3,2,1,0:T(8,128)S(1)} %bitcast.22, bf16[1,8,128,128]{3,2,1,0:T(8,128)(2,1)S(1)} %copy-done.2, ...), custom_call_target="tpu_custom_call" | custom-call | tf_op jit(solution)/shard_map/pallas_call | solution.py:297
  105.3 4.6 %all-to-all-done.3 = f32[16,128,128]{2,1,0:T(8,128)S(1)} async-done(((f32[16,128,128]{2,1,0:T(8,128)}), f32[16,128,128]{2,1,0:T(8,128)S(1)}, u32[]{:S(2)}, u32[]{:S(2)}) %all-to-all-start.3) | async-done | bytes 1048608 | tf_op jit(solution)/shard_map/all_to_all | solution.py:239
  109.9 6.6 %shard_map.100 = f32[16,2,2,8,8,128]{5,4,3,2,1,0:T(8,128)S(1)} custom-call(f32[16,2,8,8,128]{4,3,2,1,0:T(8,128)S(1)} %bitcast.20, bf16[1,8,128,128]{3,2,1,0:T(8,128)(2,1)S(1)} %copy-done.2, f32[2,8,128,128]{3,2,1,0:T(8,128)S(1)} %shard_map.99.base_ref, bf16[2,256,256]{2,1,0:T(8,128)(2,1)S(1)} %copy-done.1, bf16[2,256,256]{2,1,0:T(8,128)(2,1)S(1)} %copy-done), custom_call_target="tpu_custom_call" | custom-call | tf_op jit(solution)/shard_map/pallas_call | solution.py:318
  116.5 39.3 %all_to_all.25.pieces_ref = f32[16,256,128]{2,1,0:T(8,128)S(1)} all-to-all(f32[16,256,128]{2,1,0:T(8,128)S(1)} %bitcast.19), channel_id=1, replica_groups=mesh['band'=16,'grid'=16] {'grid'}, dimensions={0} | all-to-all | bytes 4194304 | tf_op jit(solution)/shard_map/all_to_all | solution.py:239
  155.8 2.4 %shard_map.101 = (f32[2,1,8,128,128]{4,3,2,1,0:T(8,128)}, f32[2,1,8,128,128]{4,3,2,1,0:T(8,128)}) custom-call(f32[16,256,128]{2,1,0:T(8,128)S(1)} %all_to_all.25.pieces_ref, bf16[2,256,256]{2,1,0:T(8,128)(2,1)S(1)} %copy-done.8), custom_call_target="tpu_custom_call" | custom-call | tf_op jit(solution)/shard_map/pallas_call | solution.py:329
  (37 shorter events, 1.2 us)
Async XLA Ops:
  0.6 15.4 %copy-start.1 = (bf16[2,256,256]{2,1,0:T(8,128)(2,1)S(1)}, bf16[2,256,256]{2,1,0:T(8,128)(2,1)}, u32[]{:S(2)}) copy-start(bf16[2,256,256]{2,1,0:T(8,128)(2,1)} %constant.61.clone.up_ref) | copy-start | bytes 786436
  5.7 62.0 %copy-start = (bf16[2,256,256]{2,1,0:T(8,128)(2,1)S(1)}, bf16[2,256,256]{2,1,0:T(8,128)(2,1)}, u32[]{:S(2)}) copy-start(bf16[2,256,256]{2,1,0:T(8,128)(2,1)} %constant.60.clone.down_ref) | copy-start | bytes 786436
  5.7 35.7 %all-to-all-start = ((f32[16,128,128]{2,1,0:T(8,128)}), f32[16,128,128]{2,1,0:T(8,128)S(1)}, u32[]{:S(2)}, u32[]{:S(2)}) async-start(f32[16,128,128]{2,1,0:T(8,128)} %bitcast.24), calls=%async_computation | async-start | bytes 2097152 | tf_op jit(solution)/shard_map/all_to_all | solution.py:239
  42.1 37.7 %collective-permute-start.5 = (f32[128,128]{1,0:T(8,128)S(1)}, f32[128,128]{1,0:T(8,128)S(1)}, u32[]{:S(2)}, u32[]{:S(2)}) collective-permute-start(f32[128,128]{1,0:T(8,128)S(1)} %get-tuple-element.11), channel_id=1, source_target_pairs={{0,224},{16,240},{32,192},{48,208},{64,160},{80,176},{96,128},{112... | collective-permute-start | bytes 196616 | tf_op jit(solution)/shard_map/ppermute | solution.py:243
  43.2 16.9 %collective-permute-start.2 = (f32[128,128]{1,0:T(8,128)S(1)}, f32[128,128]{1,0:T(8,128)S(1)}, u32[]{:S(2)}, u32[]{:S(2)}) collective-permute-start(f32[128,128]{1,0:T(8,128)S(1)} %get-tuple-element.11), channel_id=1, source_target_pairs={{0,128},{16,144},{32,160},{48,176},{64,192},{80,208},{96,224},{112... | collective-permute-start | bytes 196616 | tf_op jit(solution)/shard_map/ppermute | solution.py:243
  49.3 10.8 %collective-permute-start.1 = (f32[128,128]{1,0:T(8,128)S(1)}, f32[128,128]{1,0:T(8,128)S(1)}, u32[]{:S(2)}, u32[]{:S(2)}) collective-permute-start(f32[128,128]{1,0:T(8,128)S(1)} %get-tuple-element.11), channel_id=1, source_target_pairs={{0,64},{16,80},{32,96},{48,112},{64,0},{80,16},{96,32},{112,48},{1... | collective-permute-start | bytes 196616 | tf_op jit(solution)/shard_map/ppermute | solution.py:243
  49.3 10.8 %collective-permute-start = (f32[128,128]{1,0:T(8,128)S(1)}, f32[128,128]{1,0:T(8,128)S(1)}, u32[]{:S(2)}, u32[]{:S(2)}) collective-permute-start(f32[128,128]{1,0:T(8,128)S(1)} %get-tuple-element.11), channel_id=1, source_target_pairs={{0,32},{16,48},{32,0},{48,16},{64,96},{80,112},{96,64},{112,80},{1... | collective-permute-start | bytes 196616 | tf_op jit(solution)/shard_map/ppermute | solution.py:243
  49.7 18.0 %all-to-all-start.1 = ((f32[16,16,128]{2,1,0:T(8,128)}), f32[16,16,128]{2,1,0:T(8,128)S(1)}, u32[]{:S(2)}, u32[]{:S(2)}) async-start(f32[16,16,128]{2,1,0:T(8,128)} %get-tuple-element.10), calls=%async_computation.1 | async-start | bytes 262144 | tf_op jit(solution)/shard_map/all_to_all | solution.py:239
  68.8 11.2 %all-to-all-start.2 = ((f32[16,8,128]{2,1,0:T(8,128)}), f32[16,8,128]{2,1,0:T(8,128)S(1)}, u32[]{:S(2)}, u32[]{:S(2)}) async-start(f32[16,8,128]{2,1,0:T(8,128)} %shard_map.97), calls=%async_computation.2 | async-start | bytes 131072 | tf_op jit(solution)/shard_map/all_to_all | solution.py:239
  72.6 7.2 %collective-permute-start.4 = (f32[128,128]{1,0:T(8,128)S(1)}, f32[128,128]{1,0:T(8,128)S(1)}, u32[]{:S(2)}, u32[]{:S(2)}) collective-permute-start(f32[128,128]{1,0:T(8,128)S(1)} %collective-permute-done.2), channel_id=1, source_target_pairs={{0,64},{16,80},{32,96},{48,112},{64,0},{80,16},{96,32},{112,48},{1... | collective-permute-start | bytes 196616 | tf_op jit(solution)/shard_map/ppermute | solution.py:243
  73.5 25.7 %copy-start.2 = (bf16[1,8,128,128]{3,2,1,0:T(8,128)(2,1)S(1)}, bf16[1,8,128,128]{3,2,1,0:T(8,128)(2,1)}, u32[]{:S(2)}) copy-start(bf16[1,8,128,128]{3,2,1,0:T(8,128)(2,1)} %orbital_ref.5) | copy-start | bytes 786436
  73.6 25.7 %copy-start.3 = (bf16[2,1,8,128,128]{4,3,2,1,0:T(8,128)(2,1)S(1)}, bf16[2,1,8,128,128]{4,3,2,1,0:T(8,128)(2,1)}, u32[]{:S(2)}) copy-start(bf16[2,1,8,128,128]{4,3,2,1,0:T(8,128)(2,1)} %trial_ref.3) | copy-start | bytes 1572868
  73.6 6.1 %collective-permute-start.3 = (f32[2,128,128]{2,1,0:T(8,128)S(1)}, f32[2,128,128]{2,1,0:T(8,128)S(1)}, u32[]{:S(2)}, u32[]{:S(2)}) collective-permute-start(f32[2,128,128]{2,1,0:T(8,128)S(1)} %pad_maximum_fusion), channel_id=1, source_target_pairs={{0,32},{16,48},{32,0},{48,16},{64,96},{80,112},{96,64},{112,80},{1... | collective-permute-start | bytes 393224 | tf_op jit(solution)/shard_map/ppermute | solution.py:243
  79.8 19.5 %copy-start.4 = (f32[8,128,128]{2,1,0:T(8,128)}, f32[8,128,128]{2,1,0:T(8,128)S(1)}, u32[]{:S(2)}) copy-start(f32[8,128,128]{2,1,0:T(8,128)S(1)} %bitcast_dynamic-update-slice_fusion) | copy-start | bytes 1572868
  81.1 28.9 %all-to-all-start.3 = ((f32[16,128,128]{2,1,0:T(8,128)}), f32[16,128,128]{2,1,0:T(8,128)S(1)}, u32[]{:S(2)}, u32[]{:S(2)}) async-start(f32[16,128,128]{2,1,0:T(8,128)} %shard_map.98), calls=%async_computation.3 | async-start | bytes 2097152 | tf_op jit(solution)/shard_map/all_to_all | solution.py:239
  84.7 14.5 %collective-permute-start.6 = (f32[8,128,128]{2,1,0:T(8,128)S(1)}, f32[8,128,128]{2,1,0:T(8,128)S(1)}, u32[]{:S(2)}, u32[]{:S(2)}) collective-permute-start(f32[8,128,128]{2,1,0:T(8,128)S(1)} %bitcast_dynamic-update-slice_fusion), channel_id=1, source_target_pairs={{0,16},{16,0},{32,48},{48,32},{64,80},{80,64},{96,112},{112,96},{1... | collective-permute-start | bytes 1572872 | tf_op jit(solution)/shard_map/ppermute | solution.py:243
  99.3 1.0 copy-start.5
  100.3 1.0 copy-start.6
  101.4 1.0 copy-start.7
  116.5 39.3 %copy-start.8 = (bf16[2,256,256]{2,1,0:T(8,128)(2,1)S(1)}, bf16[2,256,256]{2,1,0:T(8,128)(2,1)}, u32[]{:S(2)}) copy-start(bf16[2,256,256]{2,1,0:T(8,128)(2,1)} %constant.62.clone.x_ref) | copy-start | bytes 786436

commit v4 on v3

--- a/solution.py
+++ b/solution.py
@@ -279,19 +279,22 @@
     held = {0: spectrum}
     for mask in (2, 4, 8):
         held[mask] = partner(spectrum, mask)
-    lines, held[2], held[4], held[8] = lax.optimization_barrier((lines, held[2], held[4], held[8]))
     lines = call(line_kernel, (parts, share, length))(
         lines, kernel, tables["down"], own_up
     )
-    lines = exchange(lines, "grid")
+    lines, held[2], held[4], held[8] = lax.optimization_barrier((lines, held[2], held[4], held[8]))
+    lines = exchange(lines, "grid").reshape(parts * share, length)
     both = partner(jnp.stack([held[4], held[8]]), 2)
     held[6], held[10] = both[0], both[1]
     held[12] = partner(held[8], 4)
     held[14] = partner(spectrum, 14)
+    away = {}
+    for masks in ((0, 2, 4, 8), (6, 10, 12, 14)):
+        group = partner(jnp.stack([held[mask] for mask in masks]), 1)
+        for i, mask in enumerate(masks):
+            away[mask] = group[i]
     near = jnp.stack([held[mask] for mask in range(0, parts, 2)])
-    lines, near = lax.optimization_barrier((lines, near))
-    far = partner(near, 1)
-    lines = lines.reshape(parts * share, length)
+    far = jnp.stack([away[mask] for mask in range(0, parts, 2)])
     potential = call(spread_kernel, (parts, 2 * points, length))(lines)
     potential = exchange(potential, "band").reshape(parts, 2, share, share, length)
     base = call(

time: 159 us -> 165 us (1.038)
  blocking collectives: 39.3 us -> 47.5 us
  local copies, waits for them, and re-layouts: 3.22 us -> 0.14 us
  waiting for transfers between devices: 55.9 us -> 57.9 us
    ppermute x7 -> x8, waiting for transfers between devices: 18.3 us -> 28 us  [partner(): lax.ppermute(array, 'band', [(i, i ^ mask) for i in range(lax.axis_size('...]
    all_to_all x1 -> x2, blocking collectives: 39.3 us -> 47.5 us  [exchange(): return lax.all_to_all(array, axis, split_axis=0, concat_axis=0, tiled=True)]
    all_to_all x4 -> x3, waiting for transfers between devices: 37.6 us -> 30 us  [exchange(): return lax.all_to_all(array, axis, split_axis=0, concat_axis=0, tiled=True)]
    unnamed x25 -> x21, local copies, waits for them, and re-layouts: 3.2 us -> 0.08 us
    ppermute x7 -> x8, starting transfers between devices: 10.3 us -> 11.5 us  [partner(): lax.ppermute(array, 'band', [(i, i ^ mask) for i in range(lax.axis_size('...]
    all_to_all x4 -> x3, starting transfers between devices: 28 us -> 26.9 us  [exchange(): return lax.all_to_all(array, axis, split_axis=0, concat_axis=0, tiled=True)]
  transfers between devices with their start and end apart: 11 -> 11, of which waited for: 6 -> 7; matrix products, arithmetic and copies ran while one was open for 0% -> 0% of each run, Pallas kernels for 3% -> 2%
where the time goes in v4:
time: 165 us
  waiting for transfers between devices  57.9 us (35%)
  blocking collectives  47.5 us (29%)
  starting transfers between devices  38.4 us (23%)
  Pallas kernels  19.2 us (12%)
    all_to_all x2, blocking collectives, exchange(): return lax.all_to_all(array, axis, split_axis=0, concat_axis=0, tiled=True)  47.5 us
    all_to_all x3, waiting for transfers between devices, exchange(): return lax.all_to_all(array, axis, split_axis=0, concat_axis=0, tiled=True)  30 us
    ppermute x8, waiting for transfers between devices, partner(): lax.ppermute(array, 'band', [(i, i ^ mask) for i in range(lax.axis_size('...  28 us
    all_to_all x3, starting transfers between devices, exchange(): return lax.all_to_all(array, axis, split_axis=0, concat_axis=0, tiled=True)  26.9 us
    ppermute x8, starting transfers between devices, partner(): lax.ppermute(array, 'band', [(i, i ^ mask) for i in range(lax.axis_size('...  11.5 us
    pallas_call x1, Pallas kernels, per_device(): call(field_kernel, (parts, 2, 2, share, share, length), grid=steps, in_sp...  6.61 us
    pallas_call x1, Pallas kernels, per_device(): call(density_kernel, (parts, 2, share, share, length), grant=WIDE_GRANT,...  5.02 us
  transfers between devices with their start and end apart: 11, of which 7 were waited for; matrix products, arithmetic and copies ran while one was open for 0% of the time, Pallas kernels for 2%

profile of v4, /device:TPU:1, one launch (start us, length us, event | category | flops | bytes accessed | tf_op | source)
XLA Modules:
  0.0 164.9 jit_solution(5338924285920668649)
XLA Ops:
  0.6 5.0 %shard_map.95 = f32[16,2,8,8,128]{4,3,2,1,0:T(8,128)} custom-call(bf16[1,8,128,128]{3,2,1,0:T(8,128)(2,1)} %orbital_ref.5, bf16[2,1,8,128,128]{4,3,2,1,0:T(8,128)(2,1)} %trial_ref.3, bf16[2,256,256]{2,1,0:T(8,128)(2,1)} %constant.61.clone.up_ref, bf16[2,256,256]{2,1,0:T(8,128)(2,1)} %constant.60.clone.down_ref), custom_call_target="tpu_custom_call" | custom-call | tf_op jit(solution)/shard_map/pallas_call | solution.py:268
  5.7 10.3 %all-to-all-start = ((f32[16,128,128]{2,1,0:T(8,128)}), f32[16,128,128]{2,1,0:T(8,128)S(1)}, u32[]{:S(2)}, u32[]{:S(2)}) async-start(f32[16,128,128]{2,1,0:T(8,128)} %bitcast.26), calls=%async_computation | async-start | bytes 2097152 | tf_op jit(solution)/shard_map/all_to_all | solution.py:239
  16.0 25.4 %all-to-all-done.pieces_ref = f32[16,128,128]{2,1,0:T(8,128)S(1)} async-done(((f32[16,128,128]{2,1,0:T(8,128)}), f32[16,128,128]{2,1,0:T(8,128)S(1)}, u32[]{:S(2)}, u32[]{:S(2)}) %all-to-all-start) | async-done | bytes 1048608 | tf_op jit(solution)/shard_map/all_to_all | solution.py:239
  41.3 0.7 shard_map.96
  42.1 10.9 %all-to-all-start.1 = ((f32[16,16,128]{2,1,0:T(8,128)}), f32[16,16,128]{2,1,0:T(8,128)S(1)}, u32[]{:S(2)}, u32[]{:S(2)}) async-start(f32[16,16,128]{2,1,0:T(8,128)} %get-tuple-element.8), calls=%async_computation.1 | async-start | bytes 262144 | tf_op jit(solution)/shard_map/all_to_all | solution.py:239
  53.1 1.2 collective-permute-start.2
  54.3 1.7 %collective-permute-start.1 = (f32[128,128]{1,0:T(8,128)S(1)}, f32[128,128]{1,0:T(8,128)S(1)}, u32[]{:S(2)}, u32[]{:S(2)}) collective-permute-start(f32[128,128]{1,0:T(8,128)S(1)} %get-tuple-element.9), channel_id=1, source_target_pairs={{0,64},{16,80},{32,96},{48,112},{64,0},{80,16},{96,32},{112,48},{1... | collective-permute-start | bytes 196616 | tf_op jit(solution)/shard_map/ppermute | solution.py:243
  56.0 4.6 %all-to-all-done.1.pieces_ref = f32[16,16,128]{2,1,0:T(8,128)S(1)} async-done(((f32[16,16,128]{2,1,0:T(8,128)}), f32[16,16,128]{2,1,0:T(8,128)S(1)}, u32[]{:S(2)}, u32[]{:S(2)}) %all-to-all-start.1) | async-done | bytes 131104 | tf_op jit(solution)/shard_map/all_to_all | solution.py:239
  61.1 0.9 collective-permute-done.1
  62.0 14.5 %all_to_all.25 = f32[16,8,128]{2,1,0:T(8,128)S(1)} all-to-all(f32[16,8,128]{2,1,0:T(8,128)S(1)} %shard_map.97), channel_id=1, replica_groups=mesh['band'=16,'grid'=16] {'grid'}, dimensions={0} | all-to-all | bytes 131072 | tf_op jit(solution)/shard_map/all_to_all | solution.py:239
  76.5 1.1 shard_map.98
  77.6 5.8 %all-to-all-start.3 = ((f32[16,128,128]{2,1,0:T(8,128)}), f32[16,128,128]{2,1,0:T(8,128)S(1)}, u32[]{:S(2)}, u32[]{:S(2)}) async-start(f32[16,128,128]{2,1,0:T(8,128)} %shard_map.98), calls=%async_computation.3 | async-start | bytes 2097152 | tf_op jit(solution)/shard_map/all_to_all | solution.py:239
  84.0 2.7 %collective-permute-start.5 = (f32[128,128]{1,0:T(8,128)S(1)}, f32[128,128]{1,0:T(8,128)S(1)}, u32[]{:S(2)}, u32[]{:S(2)}) collective-permute-start(f32[128,128]{1,0:T(8,128)S(1)} %get-tuple-element.9), channel_id=1, source_target_pairs={{0,224},{16,240},{32,192},{48,208},{64,160},{80,176},{96,128},{112... | collective-permute-start | bytes 196616 | tf_op jit(solution)/shard_map/ppermute | solution.py:243
  86.7 3.0 %collective-permute-start.4 = (f32[128,128]{1,0:T(8,128)S(1)}, f32[128,128]{1,0:T(8,128)S(1)}, u32[]{:S(2)}, u32[]{:S(2)}) collective-permute-start(f32[128,128]{1,0:T(8,128)S(1)} %collective-permute-done.2), channel_id=1, source_target_pairs={{0,64},{16,80},{32,96},{48,112},{64,0},{80,16},{96,32},{112,48},{1... | collective-permute-start | bytes 196616 | tf_op jit(solution)/shard_map/ppermute | solution.py:243
  90.1 1.3 collective-permute-start.6
  91.4 18.3 %collective-permute-done.5 = f32[128,128]{1,0:T(8,128)S(1)} collective-permute-done((f32[128,128]{1,0:T(8,128)S(1)}, f32[128,128]{1,0:T(8,128)S(1)}, u32[]{:S(2)}, u32[]{:S(2)}) %collective-permute-start.5) | collective-permute-done | bytes 65568 | tf_op jit(solution)/shard_map/ppermute | solution.py:243
  109.7 0.9 collective-permute-done.4
  110.6 2.7 %collective-permute-done.3 = f32[2,128,128]{2,1,0:T(8,128)S(1)} collective-permute-done((f32[2,128,128]{2,1,0:T(8,128)S(1)}, f32[2,128,128]{2,1,0:T(8,128)S(1)}, u32[]{:S(2)}, u32[]{:S(2)}) %collective-permute-start.3) | collective-permute-done | bytes 131104 | tf_op jit(solution)/shard_map/ppermute | solution.py:243
  113.3 1.3 collective-permute-start.7
  114.7 5.2 %collective-permute-done.7 = f32[4,128,128]{2,1,0:T(8,128)S(1)} collective-permute-done((f32[4,128,128]{2,1,0:T(8,128)S(1)}, f32[4,128,128]{2,1,0:T(8,128)S(1)}, u32[]{:S(2)}, u32[]{:S(2)}) %collective-permute-start.7) | collective-permute-done | bytes 262176 | tf_op jit(solution)/shard_map/ppermute | solution.py:243
  120.0 2.9 %shard_map.99.base_ref = f32[2,8,128,128]{3,2,1,0:T(8,128)S(1)} custom-call(s32[1]{0:T(128)} %bitcast.3.me_ref, f32[1]{0:T(128)S(6)} %copy.17.energy_ref, f32[8,2,8,8,128]{4,3,2,1,0:T(8,128)S(1)} %constant_dynamic-update-slice_fusion.near_ref, f32[8,2,8,8,128]{4,3,2,1,0:T(8,128)S(1)} %bitcast.22, bf16[1,8,128,128]{3,2,1,0:T(8,128)(2,1)S(1)} %copy-done.2, ...), custom_call_target="tpu_custom_call" | custom-call | tf_op jit(solution)/shard_map/pallas_call | solution.py:300
  122.9 6.6 %shard_map.100 = f32[16,2,2,8,8,128]{5,4,3,2,1,0:T(8,128)S(1)} custom-call(f32[16,2,8,8,128]{4,3,2,1,0:T(8,128)S(1)} %bitcast.21, bf16[1,8,128,128]{3,2,1,0:T(8,128)(2,1)S(1)} %copy-done.2, f32[2,8,128,128]{3,2,1,0:T(8,128)S(1)} %shard_map.99.base_ref, bf16[2,256,256]{2,1,0:T(8,128)(2,1)S(1)} %copy-done.1, bf16[2,256,256]{2,1,0:T(8,128)(2,1)S(1)} %copy-done), custom_call_target="tpu_custom_call" | custom-call | tf_op jit(solution)/shard_map/pallas_call | solution.py:321
  129.5 33.0 %all_to_all.26.pieces_ref = f32[16,256,128]{2,1,0:T(8,128)S(1)} all-to-all(f32[16,256,128]{2,1,0:T(8,128)S(1)} %bitcast.20), channel_id=1, replica_groups=mesh['band'=16,'grid'=16] {'grid'}, dimensions={0} | all-to-all | bytes 4194304 | tf_op jit(solution)/shard_map/all_to_all | solution.py:239
  162.5 2.4 %shard_map.101 = (f32[2,1,8,128,128]{4,3,2,1,0:T(8,128)}, f32[2,1,8,128,128]{4,3,2,1,0:T(8,128)}) custom-call(f32[16,256,128]{2,1,0:T(8,128)S(1)} %all_to_all.26.pieces_ref, bf16[2,256,256]{2,1,0:T(8,128)(2,1)S(1)} %copy-done.6), custom_call_target="tpu_custom_call" | custom-call | tf_op jit(solution)/shard_map/pallas_call | solution.py:332
  (42 shorter events, 1.2 us)
Async XLA Ops:
  5.7 50.4 %copy-start.1 = (bf16[2,256,256]{2,1,0:T(8,128)(2,1)S(1)}, bf16[2,256,256]{2,1,0:T(8,128)(2,1)}, u32[]{:S(2)}) copy-start(bf16[2,256,256]{2,1,0:T(8,128)(2,1)} %constant.61.clone.up_ref) | copy-start | bytes 786436
  5.7 55.0 %copy-start = (bf16[2,256,256]{2,1,0:T(8,128)(2,1)S(1)}, bf16[2,256,256]{2,1,0:T(8,128)(2,1)}, u32[]{:S(2)}) copy-start(bf16[2,256,256]{2,1,0:T(8,128)(2,1)} %constant.60.clone.down_ref) | copy-start | bytes 786436
  5.7 35.7 %all-to-all-start = ((f32[16,128,128]{2,1,0:T(8,128)}), f32[16,128,128]{2,1,0:T(8,128)S(1)}, u32[]{:S(2)}, u32[]{:S(2)}) async-start(f32[16,128,128]{2,1,0:T(8,128)} %bitcast.26), calls=%async_computation | async-start | bytes 2097152 | tf_op jit(solution)/shard_map/all_to_all | solution.py:239
  42.1 18.6 %all-to-all-start.1 = ((f32[16,16,128]{2,1,0:T(8,128)}), f32[16,16,128]{2,1,0:T(8,128)S(1)}, u32[]{:S(2)}, u32[]{:S(2)}) async-start(f32[16,16,128]{2,1,0:T(8,128)} %get-tuple-element.8), calls=%async_computation.1 | async-start | bytes 262144 | tf_op jit(solution)/shard_map/all_to_all | solution.py:239
  53.1 8.0 %collective-permute-start.2 = (f32[128,128]{1,0:T(8,128)S(1)}, f32[128,128]{1,0:T(8,128)S(1)}, u32[]{:S(2)}, u32[]{:S(2)}) collective-permute-start(f32[128,128]{1,0:T(8,128)S(1)} %get-tuple-element.9), channel_id=1, source_target_pairs={{0,128},{16,144},{32,160},{48,176},{64,192},{80,208},{96,224},{112... | collective-permute-start | bytes 196616 | tf_op jit(solution)/shard_map/ppermute | solution.py:243
  54.3 7.7 %collective-permute-start.1 = (f32[128,128]{1,0:T(8,128)S(1)}, f32[128,128]{1,0:T(8,128)S(1)}, u32[]{:S(2)}, u32[]{:S(2)}) collective-permute-start(f32[128,128]{1,0:T(8,128)S(1)} %get-tuple-element.9), channel_id=1, source_target_pairs={{0,64},{16,80},{32,96},{48,112},{64,0},{80,16},{96,32},{112,48},{1... | collective-permute-start | bytes 196616 | tf_op jit(solution)/shard_map/ppermute | solution.py:243
  56.0 6.0 %collective-permute-start = (f32[128,128]{1,0:T(8,128)S(1)}, f32[128,128]{1,0:T(8,128)S(1)}, u32[]{:S(2)}, u32[]{:S(2)}) collective-permute-start(f32[128,128]{1,0:T(8,128)S(1)} %get-tuple-element.9), channel_id=1, source_target_pairs={{0,32},{16,48},{32,0},{48,16},{64,96},{80,112},{96,64},{112,80},{1... | collective-permute-start | bytes 196616 | tf_op jit(solution)/shard_map/ppermute | solution.py:243
  77.6 45.3 %all-to-all-start.3 = ((f32[16,128,128]{2,1,0:T(8,128)}), f32[16,128,128]{2,1,0:T(8,128)S(1)}, u32[]{:S(2)}, u32[]{:S(2)}) async-start(f32[16,128,128]{2,1,0:T(8,128)} %shard_map.98), calls=%async_computation.3 | async-start | bytes 2097152 | tf_op jit(solution)/shard_map/all_to_all | solution.py:239
  84.0 25.6 %collective-permute-start.5 = (f32[128,128]{1,0:T(8,128)S(1)}, f32[128,128]{1,0:T(8,128)S(1)}, u32[]{:S(2)}, u32[]{:S(2)}) collective-permute-start(f32[128,128]{1,0:T(8,128)S(1)} %get-tuple-element.9), channel_id=1, source_target_pairs={{0,224},{16,240},{32,192},{48,208},{64,160},{80,176},{96,128},{112... | collective-permute-start | bytes 196616 | tf_op jit(solution)/shard_map/ppermute | solution.py:243
  86.7 23.9 %collective-permute-start.4 = (f32[128,128]{1,0:T(8,128)S(1)}, f32[128,128]{1,0:T(8,128)S(1)}, u32[]{:S(2)}, u32[]{:S(2)}) collective-permute-start(f32[128,128]{1,0:T(8,128)S(1)} %collective-permute-done.2), channel_id=1, source_target_pairs={{0,64},{16,80},{32,96},{48,112},{64,0},{80,16},{96,32},{112,48},{1... | collective-permute-start | bytes 196616 | tf_op jit(solution)/shard_map/ppermute | solution.py:243
  89.7 23.6 %collective-permute-start.3 = (f32[2,128,128]{2,1,0:T(8,128)S(1)}, f32[2,128,128]{2,1,0:T(8,128)S(1)}, u32[]{:S(2)}, u32[]{:S(2)}) collective-permute-start(f32[2,128,128]{2,1,0:T(8,128)S(1)} %pad_maximum_fusion.3), channel_id=1, source_target_pairs={{0,32},{16,48},{32,0},{48,16},{64,96},{80,112},{96,64},{112,80},{1... | collective-permute-start | bytes 393224 | tf_op jit(solution)/shard_map/ppermute | solution.py:243
  90.1 29.9 %copy-start.2 = (bf16[1,8,128,128]{3,2,1,0:T(8,128)(2,1)S(1)}, bf16[1,8,128,128]{3,2,1,0:T(8,128)(2,1)}, u32[]{:S(2)}) copy-start(bf16[1,8,128,128]{3,2,1,0:T(8,128)(2,1)} %orbital_ref.5) | copy-start | bytes 786436
  90.1 29.9 %copy-start.3 = (bf16[2,1,8,128,128]{4,3,2,1,0:T(8,128)(2,1)S(1)}, bf16[2,1,8,128,128]{4,3,2,1,0:T(8,128)(2,1)}, u32[]{:S(2)}) copy-start(bf16[2,1,8,128,128]{4,3,2,1,0:T(8,128)(2,1)} %trial_ref.3) | copy-start | bytes 1572868
  90.1 29.9 %copy-start.4 = (f32[8,128,128]{2,1,0:T(8,128)S(1)}, f32[8,128,128]{2,1,0:T(8,128)}, u32[]{:S(2)}) copy-start(f32[8,128,128]{2,1,0:T(8,128)} %alda_ref.1) | copy-start | bytes 1572868
  90.1 29.9 %copy-start.5 = (f32[8,128,128]{2,1,0:T(8,128)S(1)}, f32[8,128,128]{2,1,0:T(8,128)}, u32[]{:S(2)}) copy-start(f32[8,128,128]{2,1,0:T(8,128)} %local_ref.1) | copy-start | bytes 1572868
  90.1 24.6 %collective-permute-start.6 = (f32[4,128,128]{2,1,0:T(8,128)S(1)}, f32[4,128,128]{2,1,0:T(8,128)S(1)}, u32[]{:S(2)}, u32[]{:S(2)}) collective-permute-start(f32[4,128,128]{2,1,0:T(8,128)S(1)} %pad_maximum_fusion.1), channel_id=1, source_target_pairs={{0,16},{16,0},{32,48},{48,32},{64,80},{80,64},{96,112},{112,96},{1... | collective-permute-start | bytes 786440 | tf_op jit(solution)/shard_map/ppermute | solution.py:243
  113.3 6.6 %collective-permute-start.7 = (f32[4,128,128]{2,1,0:T(8,128)S(1)}, f32[4,128,128]{2,1,0:T(8,128)S(1)}, u32[]{:S(2)}, u32[]{:S(2)}) collective-permute-start(f32[4,128,128]{2,1,0:T(8,128)S(1)} %pad_maximum_fusion.2), channel_id=1, source_target_pairs={{0,16},{16,0},{32,48},{48,32},{64,80},{80,64},{96,112},{112,96},{1... | collective-permute-start | bytes 786440 | tf_op jit(solution)/shard_map/ppermute | solution.py:243
  129.5 33.0 %copy-start.6 = (bf16[2,256,256]{2,1,0:T(8,128)(2,1)S(1)}, bf16[2,256,256]{2,1,0:T(8,128)(2,1)}, u32[]{:S(2)}) copy-start(bf16[2,256,256]{2,1,0:T(8,128)(2,1)} %constant.62.clone.x_ref) | copy-start | bytes 786436

commit v5 on v4

--- a/solution.py
+++ b/solution.py
@@ -13,7 +13,7 @@
 box_length = 30.0
 NARROW = jnp.bfloat16
 WIDE = jnp.float32
-ROWS = 2
+ROWS = 8
 GRANT = 20 * 2**20
 WIDE_GRANT = 60 * 2**20
 
@@ -72,23 +72,52 @@
     return jnp.concatenate([value[:half], value[half:]], axis=1)
 
 
-def density_kernel(orbital_ref, trial_ref, up_ref, down_ref, out_ref):
+def density_kernel(orbital_in, trial_in, up_in, down_in, out_hbm, *scratch):
+    orbital_ref, trial_ref, up_ref, down_ref, out_ref, table_sems, row_sems, out_sems = scratch
     length = orbital_ref.shape[2]
     parts, share = out_ref.shape[0], out_ref.shape[3]
-    rows = orbital_ref.shape[1]
-    values = []
-    for x in range(rows):
-        orbital = 2.0 * orbital_ref[0, x].astype(WIDE)
-        values.append(
-            jnp.concatenate([trial_ref[k, 0, x].astype(WIDE) * orbital for k in range(2)], axis=1)
+    half = orbital_ref.shape[1] // 2
+    tables = [
+        pltpu.make_async_copy(up_in, up_ref, table_sems.at[0]),
+        pltpu.make_async_copy(down_in, down_ref, table_sems.at[1]),
+    ]
+    rows = [pl.ds(i * half, half) for i in range(2)]
+    orbitals, trials, outs = [], [], []
+    for i in range(2):
+        part = (slice(None), rows[i])
+        orbitals.append(
+            pltpu.make_async_copy(orbital_in.at[part], orbital_ref.at[part], row_sems.at[i, 0])
         )
-    turned = product(split(jnp.concatenate(values, axis=0)), pair(up_ref))
-    columns = [parts_down(turned[x * length : (x + 1) * length]) for x in range(rows)]
-    turned = product(pair(down_ref), split(jnp.concatenate(columns, axis=1)))
-    for x in range(rows):
-        for part in range(2):
-            block = turned[part * length : (part + 1) * length, x * length : (x + 1) * length]
-            out_ref[:, part, x] = block.reshape(parts, share, length)
+        part = (slice(None), slice(None), rows[i])
+        trials.append(
+            pltpu.make_async_copy(trial_in.at[part], trial_ref.at[part], row_sems.at[i, 1])
+        )
+        outs.append(pltpu.make_async_copy(out_ref.at[part], out_hbm.at[part], out_sems.at[i]))
+    for copy in (tables[0], orbitals[0], trials[0], tables[1], orbitals[1], trials[1]):
+        copy.start()
+    for copy in tables:
+        copy.wait()
+    for i in range(2):
+        orbitals[i].wait()
+        trials[i].wait()
+        values = []
+        for x in range(half):
+            orbital = 2.0 * orbital_ref[0, i * half + x].astype(WIDE)
+            values.append(
+                jnp.concatenate(
+                    [trial_ref[k, 0, i * half + x].astype(WIDE) * orbital for k in range(2)], axis=1
+                )
+            )
+        turned = product(split(jnp.concatenate(values, axis=0)), pair(up_ref))
+        columns = [parts_down(turned[x * length : (x + 1) * length]) for x in range(half)]
+        turned = product(pair(down_ref), split(jnp.concatenate(columns, axis=1)))
+        for x in range(half):
+            for part in range(2):
+                block = turned[part * length : (part + 1) * length, x * length : (x + 1) * length]
+                out_ref[:, part, i * half + x] = block.reshape(parts, share, length)
+        outs[i].start()
+    for copy in outs:
+        copy.wait()
 
 
 def share_kernel(pieces_ref, share_ref, out_ref):
@@ -265,13 +294,24 @@
     base_block = pl.BlockSpec((2, ROWS, length, length), lambda i: (0, i, 0, 0))
     steps = (share // ROWS,)
 
+    held = pl.BlockSpec(memory_space=pltpu.HBM)
+    shape = (parts, 2, share, share, length)
     pieces = call(
         density_kernel,
-        (parts, 2, share, share, length),
+        shape,
         grant=WIDE_GRANT,
-        grid=steps,
-        in_specs=[orbital_block, trial_block, table_block, table_block],
-        out_specs=share_block,
+        in_specs=[held] * 4,
+        out_specs=held,
+        scratch_shapes=[
+            pltpu.VMEM(orbitals.shape, NARROW),
+            pltpu.VMEM(trials.shape, NARROW),
+            pltpu.VMEM(tables["up"].shape, NARROW),
+            pltpu.VMEM(tables["down"].shape, NARROW),
+            pltpu.VMEM(shape, WIDE),
+            pltpu.SemaphoreType.DMA((2,)),
+            pltpu.SemaphoreType.DMA((2, 2)),
+            pltpu.SemaphoreType.DMA((2,)),
+        ],
     )(orbitals, trials, tables["up"], tables["down"])
     pieces = exchange(pieces.reshape(parts, 2 * points, length), "band")
     spectrum, lines = call(share_kernel, [(2 * points, length), (parts, 2 * share, length)])(pieces)

time: 165 us -> 160 us (0.970)
  Pallas kernels: 19.2 us -> 13.6 us
    pallas_call x1, Pallas kernels: 6.61 us -> 3.78 us  [per_device(): call(field_kernel, (parts, 2, 2, share, share, length), grid=steps, in_sp...]
    pallas_call x1, Pallas kernels: 2.9 us -> 1.05 us  [per_device(): call(base_kernel, (2, share, length, length), grid=steps, in_specs=[scala...]
  transfers between devices with their start and end apart: 11 -> 11, of which waited for: 7 -> 7; matrix products, arithmetic and copies ran while one was open for 0% -> 0% of each run, Pallas kernels for 2% -> 1%
where the time goes in v5:
time: 160 us; the launch traced here: 159 us
  waiting for transfers between devices  57.9 us (36%)
  blocking collectives  47.5 us (30%)
  starting transfers between devices  38.4 us (24%)
  Pallas kernels  13.6 us (8%)
    all_to_all x2, blocking collectives, exchange(): return lax.all_to_all(array, axis, split_axis=0, concat_axis=0, tiled=True)  47.5 us
    all_to_all x3, waiting for transfers between devices, exchange(): return lax.all_to_all(array, axis, split_axis=0, concat_axis=0, tiled=True)  30 us
    ppermute x8, waiting for transfers between devices, partner(): lax.ppermute(array, 'band', [(i, i ^ mask) for i in range(lax.axis_size('...  28 us
    all_to_all x3, starting transfers between devices, exchange(): return lax.all_to_all(array, axis, split_axis=0, concat_axis=0, tiled=True)  26.9 us
    ppermute x8, starting transfers between devices, partner(): lax.ppermute(array, 'band', [(i, i ^ mask) for i in range(lax.axis_size('...  11.5 us
    pallas_call x1, Pallas kernels, per_device(): call(density_kernel, shape, grant=WIDE_GRANT, in_specs=[held] * 4, out_sp...  4.14 us
    pallas_call x1, Pallas kernels, per_device(): call(field_kernel, (parts, 2, 2, share, share, length), grid=steps, in_sp...  3.78 us
  transfers between devices with their start and end apart: 11, of which 7 were waited for; matrix products, arithmetic and copies ran while one was open for 0% of the time, Pallas kernels for 1%

profile of v5, /device:TPU:1, one launch (start us, length us, event | category | flops | bytes accessed | tf_op | source)
XLA Modules:
  0.0 159.4 jit_solution(14118165581802765403)
XLA Ops:
  0.6 4.1 %shard_map.95 = f32[16,2,8,8,128]{4,3,2,1,0:T(8,128)} custom-call(bf16[1,8,128,128]{3,2,1,0:T(8,128)(2,1)} %orbital_ref.3, bf16[2,1,8,128,128]{4,3,2,1,0:T(8,128)(2,1)} %trial_ref.1, bf16[2,256,256]{2,1,0:T(8,128)(2,1)} %constant.61.clone.up_in.up_ref, bf16[2,256,256]{2,1,0:T(8,128)(2,1)} %constant.60.clone.down_in.down_ref), custom_call_target="tpu_custom_call" | custom-call | tf_op jit(solution)/shard_map/pallas_call | solution.py:299
  4.8 10.3 %all-to-all-start = ((f32[16,128,128]{2,1,0:T(8,128)}), f32[16,128,128]{2,1,0:T(8,128)S(1)}, u32[]{:S(2)}, u32[]{:S(2)}) async-start(f32[16,128,128]{2,1,0:T(8,128)} %bitcast.26), calls=%async_computation | async-start | bytes 2097152 | tf_op jit(solution)/shard_map/all_to_all | solution.py:268
  15.1 25.4 %all-to-all-done.pieces_ref = f32[16,128,128]{2,1,0:T(8,128)S(1)} async-done(((f32[16,128,128]{2,1,0:T(8,128)}), f32[16,128,128]{2,1,0:T(8,128)S(1)}, u32[]{:S(2)}, u32[]{:S(2)}) %all-to-all-start) | async-done | bytes 1048608 | tf_op jit(solution)/shard_map/all_to_all | solution.py:268
  40.5 0.7 shard_map.96
  41.2 10.9 %all-to-all-start.1 = ((f32[16,16,128]{2,1,0:T(8,128)}), f32[16,16,128]{2,1,0:T(8,128)S(1)}, u32[]{:S(2)}, u32[]{:S(2)}) async-start(f32[16,16,128]{2,1,0:T(8,128)} %get-tuple-element.8), calls=%async_computation.1 | async-start | bytes 262144 | tf_op jit(solution)/shard_map/all_to_all | solution.py:268
  52.3 1.2 collective-permute-start.2
  53.4 1.7 %collective-permute-start.1 = (f32[128,128]{1,0:T(8,128)S(1)}, f32[128,128]{1,0:T(8,128)S(1)}, u32[]{:S(2)}, u32[]{:S(2)}) collective-permute-start(f32[128,128]{1,0:T(8,128)S(1)} %get-tuple-element.9), channel_id=1, source_target_pairs={{0,64},{16,80},{32,96},{48,112},{64,0},{80,16},{96,32},{112,48},{1... | collective-permute-start | bytes 196616 | tf_op jit(solution)/shard_map/ppermute | solution.py:272
  55.2 4.6 %all-to-all-done.1.pieces_ref = f32[16,16,128]{2,1,0:T(8,128)S(1)} async-done(((f32[16,16,128]{2,1,0:T(8,128)}), f32[16,16,128]{2,1,0:T(8,128)S(1)}, u32[]{:S(2)}, u32[]{:S(2)}) %all-to-all-start.1) | async-done | bytes 131104 | tf_op jit(solution)/shard_map/all_to_all | solution.py:268
  60.3 0.9 collective-permute-done.1
  61.2 14.5 %all_to_all.25 = f32[16,8,128]{2,1,0:T(8,128)S(1)} all-to-all(f32[16,8,128]{2,1,0:T(8,128)S(1)} %shard_map.97), channel_id=1, replica_groups=mesh['band'=16,'grid'=16] {'grid'}, dimensions={0} | all-to-all | bytes 131072 | tf_op jit(solution)/shard_map/all_to_all | solution.py:268
  75.7 1.1 shard_map.98
  76.8 5.8 %all-to-all-start.3 = ((f32[16,128,128]{2,1,0:T(8,128)}), f32[16,128,128]{2,1,0:T(8,128)S(1)}, u32[]{:S(2)}, u32[]{:S(2)}) async-start(f32[16,128,128]{2,1,0:T(8,128)} %shard_map.98), calls=%async_computation.3 | async-start | bytes 2097152 | tf_op jit(solution)/shard_map/all_to_all | solution.py:268
  83.2 2.7 %collective-permute-start.5 = (f32[128,128]{1,0:T(8,128)S(1)}, f32[128,128]{1,0:T(8,128)S(1)}, u32[]{:S(2)}, u32[]{:S(2)}) collective-permute-start(f32[128,128]{1,0:T(8,128)S(1)} %get-tuple-element.9), channel_id=1, source_target_pairs={{0,224},{16,240},{32,192},{48,208},{64,160},{80,176},{96,128},{112... | collective-permute-start | bytes 196616 | tf_op jit(solution)/shard_map/ppermute | solution.py:272
  85.9 3.0 %collective-permute-start.4 = (f32[128,128]{1,0:T(8,128)S(1)}, f32[128,128]{1,0:T(8,128)S(1)}, u32[]{:S(2)}, u32[]{:S(2)}) collective-permute-start(f32[128,128]{1,0:T(8,128)S(1)} %collective-permute-done.2), channel_id=1, source_target_pairs={{0,64},{16,80},{32,96},{48,112},{64,0},{80,16},{96,32},{112,48},{1... | collective-permute-start | bytes 196616 | tf_op jit(solution)/shard_map/ppermute | solution.py:272
  89.3 1.3 collective-permute-start.6
  90.5 18.3 %collective-permute-done.5 = f32[128,128]{1,0:T(8,128)S(1)} collective-permute-done((f32[128,128]{1,0:T(8,128)S(1)}, f32[128,128]{1,0:T(8,128)S(1)}, u32[]{:S(2)}, u32[]{:S(2)}) %collective-permute-start.5) | collective-permute-done | bytes 65568 | tf_op jit(solution)/shard_map/ppermute | solution.py:272
  108.8 0.9 collective-permute-done.4
  109.8 2.7 %collective-permute-done.3 = f32[2,128,128]{2,1,0:T(8,128)S(1)} collective-permute-done((f32[2,128,128]{2,1,0:T(8,128)S(1)}, f32[2,128,128]{2,1,0:T(8,128)S(1)}, u32[]{:S(2)}, u32[]{:S(2)}) %collective-permute-start.3) | collective-permute-done | bytes 131104 | tf_op jit(solution)/shard_map/ppermute | solution.py:272
  112.5 1.3 collective-permute-start.7
  113.9 5.2 %collective-permute-done.7 = f32[4,128,128]{2,1,0:T(8,128)S(1)} collective-permute-done((f32[4,128,128]{2,1,0:T(8,128)S(1)}, f32[4,128,128]{2,1,0:T(8,128)S(1)}, u32[]{:S(2)}, u32[]{:S(2)}) %collective-permute-start.7) | collective-permute-done | bytes 262176 | tf_op jit(solution)/shard_map/ppermute | solution.py:272
  119.2 1.1 shard_map.99.base_ref
  120.2 3.8 %shard_map.100 = f32[16,2,2,8,8,128]{5,4,3,2,1,0:T(8,128)S(1)} custom-call(f32[16,2,8,8,128]{4,3,2,1,0:T(8,128)S(1)} %bitcast.21, bf16[1,8,128,128]{3,2,1,0:T(8,128)(2,1)S(1)} %copy-done.2, f32[2,8,128,128]{3,2,1,0:T(8,128)S(1)} %shard_map.99.base_ref, bf16[2,256,256]{2,1,0:T(8,128)(2,1)S(1)} %copy-done.1, bf16[2,256,256]{2,1,0:T(8,128)(2,1)S(1)} %copy-done), custom_call_target="tpu_custom_call" | custom-call | tf_op jit(solution)/shard_map/pallas_call | solution.py:361
  124.0 33.0 %all_to_all.26.pieces_ref = f32[16,256,128]{2,1,0:T(8,128)S(1)} all-to-all(f32[16,256,128]{2,1,0:T(8,128)S(1)} %bitcast.20), channel_id=1, replica_groups=mesh['band'=16,'grid'=16] {'grid'}, dimensions={0} | all-to-all | bytes 4194304 | tf_op jit(solution)/shard_map/all_to_all | solution.py:268
  157.0 2.4 %shard_map.101 = (f32[2,1,8,128,128]{4,3,2,1,0:T(8,128)}, f32[2,1,8,128,128]{4,3,2,1,0:T(8,128)}) custom-call(f32[16,256,128]{2,1,0:T(8,128)S(1)} %all_to_all.26.pieces_ref, bf16[2,256,256]{2,1,0:T(8,128)(2,1)S(1)} %copy-done.6), custom_call_target="tpu_custom_call" | custom-call | tf_op jit(solution)/shard_map/pallas_call | solution.py:372
  (42 shorter events, 1.2 us)
Async XLA Ops:
  4.8 50.4 %copy-start.1 = (bf16[2,256,256]{2,1,0:T(8,128)(2,1)S(1)}, bf16[2,256,256]{2,1,0:T(8,128)(2,1)}, u32[]{:S(2)}) copy-start(bf16[2,256,256]{2,1,0:T(8,128)(2,1)} %constant.61.clone.up_in.up_ref) | copy-start | bytes 786436
  4.8 55.0 %copy-start = (bf16[2,256,256]{2,1,0:T(8,128)(2,1)S(1)}, bf16[2,256,256]{2,1,0:T(8,128)(2,1)}, u32[]{:S(2)}) copy-start(bf16[2,256,256]{2,1,0:T(8,128)(2,1)} %constant.60.clone.down_in.down_ref) | copy-start | bytes 786436
  4.8 35.7 %all-to-all-start = ((f32[16,128,128]{2,1,0:T(8,128)}), f32[16,128,128]{2,1,0:T(8,128)S(1)}, u32[]{:S(2)}, u32[]{:S(2)}) async-start(f32[16,128,128]{2,1,0:T(8,128)} %bitcast.26), calls=%async_computation | async-start | bytes 2097152 | tf_op jit(solution)/shard_map/all_to_all | solution.py:268
  41.2 18.6 %all-to-all-start.1 = ((f32[16,16,128]{2,1,0:T(8,128)}), f32[16,16,128]{2,1,0:T(8,128)S(1)}, u32[]{:S(2)}, u32[]{:S(2)}) async-start(f32[16,16,128]{2,1,0:T(8,128)} %get-tuple-element.8), calls=%async_computation.1 | async-start | bytes 262144 | tf_op jit(solution)/shard_map/all_to_all | solution.py:268
  52.3 8.0 %collective-permute-start.2 = (f32[128,128]{1,0:T(8,128)S(1)}, f32[128,128]{1,0:T(8,128)S(1)}, u32[]{:S(2)}, u32[]{:S(2)}) collective-permute-start(f32[128,128]{1,0:T(8,128)S(1)} %get-tuple-element.9), channel_id=1, source_target_pairs={{0,128},{16,144},{32,160},{48,176},{64,192},{80,208},{96,224},{112... | collective-permute-start | bytes 196616 | tf_op jit(solution)/shard_map/ppermute | solution.py:272
  53.4 7.7 %collective-permute-start.1 = (f32[128,128]{1,0:T(8,128)S(1)}, f32[128,128]{1,0:T(8,128)S(1)}, u32[]{:S(2)}, u32[]{:S(2)}) collective-permute-start(f32[128,128]{1,0:T(8,128)S(1)} %get-tuple-element.9), channel_id=1, source_target_pairs={{0,64},{16,80},{32,96},{48,112},{64,0},{80,16},{96,32},{112,48},{1... | collective-permute-start | bytes 196616 | tf_op jit(solution)/shard_map/ppermute | solution.py:272
  55.2 6.0 %collective-permute-start = (f32[128,128]{1,0:T(8,128)S(1)}, f32[128,128]{1,0:T(8,128)S(1)}, u32[]{:S(2)}, u32[]{:S(2)}) collective-permute-start(f32[128,128]{1,0:T(8,128)S(1)} %get-tuple-element.9), channel_id=1, source_target_pairs={{0,32},{16,48},{32,0},{48,16},{64,96},{80,112},{96,64},{112,80},{1... | collective-permute-start | bytes 196616 | tf_op jit(solution)/shard_map/ppermute | solution.py:272
  76.8 43.5 %all-to-all-start.3 = ((f32[16,128,128]{2,1,0:T(8,128)}), f32[16,128,128]{2,1,0:T(8,128)S(1)}, u32[]{:S(2)}, u32[]{:S(2)}) async-start(f32[16,128,128]{2,1,0:T(8,128)} %shard_map.98), calls=%async_computation.3 | async-start | bytes 2097152 | tf_op jit(solution)/shard_map/all_to_all | solution.py:268
  83.2 25.6 %collective-permute-start.5 = (f32[128,128]{1,0:T(8,128)S(1)}, f32[128,128]{1,0:T(8,128)S(1)}, u32[]{:S(2)}, u32[]{:S(2)}) collective-permute-start(f32[128,128]{1,0:T(8,128)S(1)} %get-tuple-element.9), channel_id=1, source_target_pairs={{0,224},{16,240},{32,192},{48,208},{64,160},{80,176},{96,128},{112... | collective-permute-start | bytes 196616 | tf_op jit(solution)/shard_map/ppermute | solution.py:272
  85.9 23.9 %collective-permute-start.4 = (f32[128,128]{1,0:T(8,128)S(1)}, f32[128,128]{1,0:T(8,128)S(1)}, u32[]{:S(2)}, u32[]{:S(2)}) collective-permute-start(f32[128,128]{1,0:T(8,128)S(1)} %collective-permute-done.2), channel_id=1, source_target_pairs={{0,64},{16,80},{32,96},{48,112},{64,0},{80,16},{96,32},{112,48},{1... | collective-permute-start | bytes 196616 | tf_op jit(solution)/shard_map/ppermute | solution.py:272
  88.8 23.6 %collective-permute-start.3 = (f32[2,128,128]{2,1,0:T(8,128)S(1)}, f32[2,128,128]{2,1,0:T(8,128)S(1)}, u32[]{:S(2)}, u32[]{:S(2)}) collective-permute-start(f32[2,128,128]{2,1,0:T(8,128)S(1)} %pad_maximum_fusion.3), channel_id=1, source_target_pairs={{0,32},{16,48},{32,0},{48,16},{64,96},{80,112},{96,64},{112,80},{1... | collective-permute-start | bytes 393224 | tf_op jit(solution)/shard_map/ppermute | solution.py:272
  89.2 29.9 %copy-start.2 = (bf16[1,8,128,128]{3,2,1,0:T(8,128)(2,1)S(1)}, bf16[1,8,128,128]{3,2,1,0:T(8,128)(2,1)}, u32[]{:S(2)}) copy-start(bf16[1,8,128,128]{3,2,1,0:T(8,128)(2,1)} %orbital_ref.3) | copy-start | bytes 786436
  89.2 29.9 %copy-start.3 = (bf16[2,1,8,128,128]{4,3,2,1,0:T(8,128)(2,1)S(1)}, bf16[2,1,8,128,128]{4,3,2,1,0:T(8,128)(2,1)}, u32[]{:S(2)}) copy-start(bf16[2,1,8,128,128]{4,3,2,1,0:T(8,128)(2,1)} %trial_ref.1) | copy-start | bytes 1572868
  89.2 29.9 %copy-start.4 = (f32[8,128,128]{2,1,0:T(8,128)S(1)}, f32[8,128,128]{2,1,0:T(8,128)}, u32[]{:S(2)}) copy-start(f32[8,128,128]{2,1,0:T(8,128)} %alda_ref.1) | copy-start | bytes 1572868
  89.2 29.9 %copy-start.5 = (f32[8,128,128]{2,1,0:T(8,128)S(1)}, f32[8,128,128]{2,1,0:T(8,128)}, u32[]{:S(2)}) copy-start(f32[8,128,128]{2,1,0:T(8,128)} %local_ref.1) | copy-start | bytes 1572868
  89.3 24.6 %collective-permute-start.6 = (f32[4,128,128]{2,1,0:T(8,128)S(1)}, f32[4,128,128]{2,1,0:T(8,128)S(1)}, u32[]{:S(2)}, u32[]{:S(2)}) collective-permute-start(f32[4,128,128]{2,1,0:T(8,128)S(1)} %pad_maximum_fusion.1), channel_id=1, source_target_pairs={{0,16},{16,0},{32,48},{48,32},{64,80},{80,64},{96,112},{112,96},{1... | collective-permute-start | bytes 786440 | tf_op jit(solution)/shard_map/ppermute | solution.py:272
  112.5 6.6 %collective-permute-start.7 = (f32[4,128,128]{2,1,0:T(8,128)S(1)}, f32[4,128,128]{2,1,0:T(8,128)S(1)}, u32[]{:S(2)}, u32[]{:S(2)}) collective-permute-start(f32[4,128,128]{2,1,0:T(8,128)S(1)} %pad_maximum_fusion.2), channel_id=1, source_target_pairs={{0,16},{16,0},{32,48},{48,32},{64,80},{80,64},{96,112},{112,96},{1... | collective-permute-start | bytes 786440 | tf_op jit(solution)/shard_map/ppermute | solution.py:272
  124.0 33.0 %copy-start.6 = (bf16[2,256,256]{2,1,0:T(8,128)(2,1)S(1)}, bf16[2,256,256]{2,1,0:T(8,128)(2,1)}, u32[]{:S(2)}) copy-start(bf16[2,256,256]{2,1,0:T(8,128)(2,1)} %constant.62.clone.x_ref) | copy-start | bytes 786436
